TPU v7x, 256 devices: a whole 4x4x8 slice. The times are simulated.
256 devices in a mesh: seq: 32 (over y, x, core), tp: 8 (over z).
Axes of the slice: x: 4, y: 4, z: 8, core: 2. Of those that a mesh axis runs over, the one named last changes fastest.
Arguments:
- hidden_in: bfloat16 [2, 16384, 2560], P(None, 'seq'), may hold values from -6 to 6
- gate_proj: bfloat16 [2560, 5120], P(None, 'tp'), may hold values from -0.125 to 0.125
- value_proj: bfloat16 [2560, 5120], P(None, 'tp'), may hold values from -0.125 to 0.125
- bc_proj: bfloat16 [2560, 256], P(None, 'tp'), may hold values from -0.125 to 0.125
- step_proj: bfloat16 [2560, 80], P(None, 'tp'), may hold values from -0.125 to 0.125
- value_conv: float32 [4, 5120], P(None, 'tp'), may hold values from -3 to 3
- bc_conv: float32 [4, 256], replicated, may hold values from -3 to 3
- step_bias: float32 [80], P('tp'), may hold values from -1.5 to 0
- log_rate: float32 [80], P('tp'), as said below
- norm_gain: float32 [5120], P('tp'), may hold values from 0.25 to 1.75
Outputs:
- mixer_out: bfloat16 [2, 16384, 5120], P(None, 'seq', 'tp')
Inputs may be any that keep to these rules, and one draw needn't show every extreme that they name: log_rate lies between -1.5 - ln(16384) and 1.0 - ln(16384).
All inputs are finite; a program needn't handle non-finite values.
Results may differ from a plain program's by a relative error of at most 0.0095.
Values may be sent and summed in bfloat16 or wider, within the bound.
A program may use at most 128 MiB of HBM per device.

v0:
```python
import jax
import jax.numpy as jnp
from jax import lax
from jax.sharding import Mesh
from jax.sharding import PartitionSpec as P

DI = 5120
HEAD_DIM = 64
STATE = 128
CONV = 4
BLOCK = 64
SEQ = ("seq_0", "seq_1", "seq_2")


epsilon = 1e-05


def passed_along(block, axis, distance):
    devices = range(lax.axis_size(axis))
    route = [(i - distance, i) for i in devices if i - distance in devices]
    return lax.ppermute(block, axis, route)


def filled_with(x, identity):
    return jax.tree.map(
        lambda part, zero: jnp.zeros_like(part) + jnp.asarray(zero, part.dtype), x, identity
    )


def entering(x, axes, combine, identity, reverse):
    before = start = filled_with(x, identity)
    so_far = x
    for axis in reversed(axes):
        length, index = lax.axis_size(axis), lax.axis_index(axis)
        pieces = jax.tree.map(lambda part: lax.all_gather(part, axis), so_far)
        inside, so_far = start, start
        for k in reversed(range(length)) if reverse else range(length):
            passed = k > index if reverse else k < index
            so_far = combine(so_far, jax.tree.map(lambda part: part[k], pieces))
            inside = jax.tree.map(lambda new, old: jnp.where(passed, new, old), so_far, inside)
        before = combine(inside, before)
    return before


def conv_silu(padded, kernel, length):
    running = jnp.zeros((padded.shape[0], length, padded.shape[2]), jnp.float32)
    for tap_index in range(kernel.shape[0]):
        running = running + kernel[tap_index] * padded[:, tap_index : tap_index + length, :]
    return jax.nn.silu(running)


def block_step(carried, inputs):
    values, log_decay, step_sizes, b_rows, c_rows = inputs
    length = log_decay.shape[1]
    cumulative = jnp.cumsum(log_decay, axis=1)
    log_gap = cumulative[:, :, None, :] - cumulative[:, None, :, :]
    causal = jnp.arange(length)[:, None] >= jnp.arange(length)[None, :]
    weights_in = jnp.exp(jnp.where(causal[None, :, :, None], log_gap, -jnp.inf))
    scores = jnp.einsum("bin,bjn->bij", c_rows, b_rows, precision=lax.Precision.HIGHEST)
    mixing = scores[:, :, :, None] * weights_in * step_sizes[:, None, :, :]
    within = jnp.einsum("bijh,bjhp->bihp", mixing, values, precision=lax.Precision.HIGHEST)
    earlier = jnp.einsum("bin,bhpn->bihp", c_rows, carried, precision=lax.Precision.HIGHEST)
    earlier = earlier * jnp.exp(cumulative)[..., None]
    remain = jnp.exp(cumulative[:, -1:, :] - cumulative) * step_sizes
    added_state = jnp.einsum(
        "bjh,bjhp,bjn->bhpn", remain, values, b_rows, precision=lax.Precision.HIGHEST
    )
    updated = jnp.exp(cumulative[:, -1, :])[:, :, None, None] * carried + added_state
    return (updated, within + earlier)


def to_blocks(series, batch_size, blocks):
    return jnp.moveaxis(series.reshape((batch_size, blocks, BLOCK) + series.shape[2:]), 1, 0)


def combine(earlier, latter):
    return (earlier[0] * latter[0], latter[0][:, :, None, None] * earlier[1] + latter[1])


def on_device(
    hidden_in,
    gate_proj,
    value_proj,
    bc_proj,
    step_proj,
    value_conv,
    bc_conv,
    step_bias,
    log_rate,
    norm_gain,
):
    batch_size, length, model_width = hidden_in.shape
    heads_here = step_proj.shape[1]
    inner_here = value_proj.shape[1]
    flat_rows = hidden_in.reshape(-1, model_width)
    gate_pre = jnp.dot(flat_rows, gate_proj, preferred_element_type=jnp.float32).astype(
        jnp.bfloat16
    )
    value_pre = jnp.dot(flat_rows, value_proj, preferred_element_type=jnp.float32).astype(
        jnp.bfloat16
    )
    step_pre = jnp.dot(flat_rows, step_proj, preferred_element_type=jnp.float32)
    bc_part = jnp.dot(flat_rows, bc_proj, preferred_element_type=jnp.float32).astype(jnp.bfloat16)
    bc_pre = lax.all_gather(bc_part, "tp", axis=1, tiled=True)
    joined = jnp.concatenate([value_pre, bc_pre], axis=1).reshape(batch_size, length, -1)
    tail_rows = joined[:, length - (CONV - 1) :, :]
    before = passed_along(tail_rows, SEQ, 1)
    padded = jnp.concatenate([before, joined], axis=1).astype(jnp.float32)
    kernel = jnp.concatenate([value_conv, bc_conv], axis=1)
    mixed_in = conv_silu(padded, kernel, length)
    values = mixed_in[..., :inner_here].reshape(batch_size, length, heads_here, HEAD_DIM)
    b_rows = mixed_in[..., inner_here : inner_here + STATE]
    c_rows = mixed_in[..., inner_here + STATE :]
    step_sizes = jax.nn.softplus(step_pre.reshape(batch_size, length, heads_here) + step_bias)
    log_decay = -step_sizes * jnp.exp(log_rate)
    blocks = length // BLOCK
    initial = jnp.zeros((batch_size, heads_here, HEAD_DIM, STATE), jnp.float32)
    local_state, outputs = lax.scan(
        block_step,
        initial,
        (
            to_blocks(values, batch_size, blocks),
            to_blocks(log_decay, batch_size, blocks),
            to_blocks(step_sizes, batch_size, blocks),
            to_blocks(b_rows, batch_size, blocks),
            to_blocks(c_rows, batch_size, blocks),
        ),
    )
    within = jnp.moveaxis(outputs, 0, 1).reshape(batch_size, length, heads_here, HEAD_DIM)
    cumulative = jnp.cumsum(log_decay, axis=1)
    decays = jnp.exp(cumulative[:, -1, :])
    arrived = entering(
        (decays, local_state),
        SEQ,
        combine,
        (jnp.ones_like(decays), jnp.zeros_like(local_state)),
        False,
    )[1]
    correction = jnp.einsum("btn,bhpn->bthp", c_rows, arrived, precision=lax.Precision.HIGHEST)
    correction = correction * jnp.exp(cumulative)[..., None]
    mixed_out = (within + correction).reshape(batch_size, length, inner_here)
    gated_out = mixed_out * jax.nn.silu(
        gate_pre.reshape(batch_size, length, inner_here).astype(jnp.float32)
    )
    squares = jnp.sum(gated_out * gated_out, axis=-1, keepdims=True)
    whole_sq = lax.psum(squares, "tp")
    return (gated_out * lax.rsqrt(whole_sq / DI + epsilon) * norm_gain).astype(jnp.bfloat16)


def solution(mesh):
    split = Mesh(mesh.devices.reshape(4, 4, 2, mesh.shape["tp"]), ("seq_0", "seq_1", "seq_2", "tp"))
    placed = (
        P(None, SEQ, None),
        P(None, "tp"),
        P(None, "tp"),
        P(None, "tp"),
        P(None, "tp"),
        P(None, "tp"),
        P(),
        P("tp"),
        P("tp"),
        P("tp"),
    )
    return jax.shard_map(
        on_device, mesh=split, in_specs=placed, out_specs=P(None, SEQ, "tp"), check_vma=False
    )
```

profile of v0, /device:TPU:1, one launch (start us, length us, event | category | flops | bytes accessed | tf_op | source)
XLA Modules:
  0.0 266.5 jit_solution(15965139563152484885)
XLA Ops:
  8.5 6.2 %convolution_convert_fusion.1 = bf16[1024,640]{0,1:T(8,128)(2,1)S(1)} fusion(bf16[1024,2560]{1,0:T(8,128)(2,1)} %bitcast.229, bf16[2560,640]{1,0:T(8,128)(2,1)S(1)} %copy-done), kind=kOutput, calls=%fused_computation.57 | convolution fusion | flops 3356098560 | bytes 9830400 | tf_op jit(solution)/shard_map/dot_general | solution.py:99
  16.3 23.7 %all_gather.29 = bf16[1024,256]{0,1:T(8,128)(2,1)S(1)} all-gather(bf16[1024,32]{0,1:T(8,128)(2,1)S(1)} %convolution_convert_fusion.2), channel_id=1, replica_groups=mesh['seq_0'=4,'seq_1'=4,'seq_2'=2,'tp'=8] {'tp'}, dimensions={1}, use_global_device_ids=true | all-gather | bytes 589824 | tf_op jit(solution)/shard_map/all_gather | solution.py:104
  41.5 3.1 %copy.121 = bf16[1024,896]{1,0:T(8,128)(2,1)S(1)} copy(bf16[1024,896]{0,1:T(8,128)(2,1)} %pad_maximum_fusion) | data formatting | bytes 3670016 | tf_op jit(solution)/shard_map/reshape | solution.py:105
  44.6 10.1 %collective-permute-start = (bf16[2,3,896]{2,1,0:T(4,128)(2,1)S(1)}, bf16[2,3,896]{2,1,0:T(4,128)(2,1)S(1)}, u32[]{:S(2)}, u32[]{:S(2)}) collective-permute-start(bf16[2,3,896]{2,1,0:T(4,128)(2,1)S(1)} %slice.155), channel_id=1, source_target_pairs={{0,8},{8,16},{16,24},{24,32},{32,40},{40,48},{48,56},{56,64},{64,7... | collective-permute-start | bytes 32264 | tf_op jit(solution)/shard_map/ppermute | solution.py:21
  54.7 4.0 %fusion.102 = (f32[2,10,512]{2,1,0:T(8,128)S(1)}, f32[2,512,10]{1,2,0:T(8,128)S(1)}) fusion(f32[10]{0:T(128)S(1)} %exp.58, f32[10]{0:T(128)S(1)} %copy-done.14, bf16[2,512,2560]{2,1,0:T(8,128)(2,1)} %param.12, bf16[2560,10]{0,1:T(8,128)(2,1)S(1)} %copy-done.10), kind=kOutput, calls=%fused_computation.135 | convolution fusion | flops 52520960 | bytes 5376080 | tf_op jit(solution)/shard_map/dot_general | solution.py:102
  66.2 4.9 %reshape_reshape.3 = f32[2,8,64,10,64]{2,1,4,3,0:T(8,128)} reshape(f32[2,512,640]{1,2,0:T(8,128)} %copy.96) | data formatting | bytes 5242880 | tf_op jit(solution)/shard_map/reshape;reshape | solution.py:73
  71.2 62.0 %while.13 = (s32[]{:T(128)}, f32[2,10,64,128]{3,2,1,0:T(8,128)S(1)}, f32[8,2,64,10,64]{2,4,3,1,0:T(8,128)}, f32[8,2,64,10]{2,0,1,3:T(8,128)S(1)}, f32[8,2,64,10]...) while((s32[]{:T(128)}, ...), condition=%wide.region_2.3_spmd.clone, body=%wide.region_0.2_spmd.clone.sunk | while | flops 328471808 | bytes 6140956 | solution.py:118
  72.7 3.1 %constant_dynamic-slice_fusion.5 = f32[1,2,64,10,64]{2,0,4,3,1:T(1,128)S(1)} fusion(f32[8,2,64,10,64]{2,0,4,3,1:T(8,128)} %get-tuple-element.235, s32[]{:T(128)} %get-tuple-element.219), kind=kLoop, calls=%fused_computation.37.clone.1 | loop fusion | bytes 655364 | tf_op jit(solution)/shard_map/while/body/jit(dynamic_index_in_dim)/dynamic_slice | solution.py:118
  80.5 3.1 %constant_dynamic-slice_fusion.5 = f32[1,2,64,10,64]{2,0,4,3,1:T(1,128)S(1)} fusion(f32[8,2,64,10,64]{2,0,4,3,1:T(8,128)} %get-tuple-element.235, s32[]{:T(128)} %get-tuple-element.219), kind=kLoop, calls=%fused_computation.37.clone.1 | loop fusion | bytes 655364 | tf_op jit(solution)/shard_map/while/body/jit(dynamic_index_in_dim)/dynamic_slice | solution.py:118
  88.2 3.1 %constant_dynamic-slice_fusion.5 = f32[1,2,64,10,64]{2,0,4,3,1:T(1,128)S(1)} fusion(f32[8,2,64,10,64]{2,0,4,3,1:T(8,128)} %get-tuple-element.235, s32[]{:T(128)} %get-tuple-element.219), kind=kLoop, calls=%fused_computation.37.clone.1 | loop fusion | bytes 655364 | tf_op jit(solution)/shard_map/while/body/jit(dynamic_index_in_dim)/dynamic_slice | solution.py:118
  96.0 3.1 %constant_dynamic-slice_fusion.5 = f32[1,2,64,10,64]{2,0,4,3,1:T(1,128)S(1)} fusion(f32[8,2,64,10,64]{2,0,4,3,1:T(8,128)} %get-tuple-element.235, s32[]{:T(128)} %get-tuple-element.219), kind=kLoop, calls=%fused_computation.37.clone.1 | loop fusion | bytes 655364 | tf_op jit(solution)/shard_map/while/body/jit(dynamic_index_in_dim)/dynamic_slice | solution.py:118
  103.7 3.1 %constant_dynamic-slice_fusion.5 = f32[1,2,64,10,64]{2,0,4,3,1:T(1,128)S(1)} fusion(f32[8,2,64,10,64]{2,0,4,3,1:T(8,128)} %get-tuple-element.235, s32[]{:T(128)} %get-tuple-element.219), kind=kLoop, calls=%fused_computation.37.clone.1 | loop fusion | bytes 655364 | tf_op jit(solution)/shard_map/while/body/jit(dynamic_index_in_dim)/dynamic_slice | solution.py:118
  106.8 2.2 fusion.141
  111.5 3.1 %constant_dynamic-slice_fusion.5 = f32[1,2,64,10,64]{2,0,4,3,1:T(1,128)S(1)} fusion(f32[8,2,64,10,64]{2,0,4,3,1:T(8,128)} %get-tuple-element.235, s32[]{:T(128)} %get-tuple-element.219), kind=kLoop, calls=%fused_computation.37.clone.1 | loop fusion | bytes 655364 | tf_op jit(solution)/shard_map/while/body/jit(dynamic_index_in_dim)/dynamic_slice | solution.py:118
  114.6 2.2 fusion.141
  119.3 3.1 %constant_dynamic-slice_fusion.5 = f32[1,2,64,10,64]{2,0,4,3,1:T(1,128)S(1)} fusion(f32[8,2,64,10,64]{2,0,4,3,1:T(8,128)} %get-tuple-element.235, s32[]{:T(128)} %get-tuple-element.219), kind=kLoop, calls=%fused_computation.37.clone.1 | loop fusion | bytes 655364 | tf_op jit(solution)/shard_map/while/body/jit(dynamic_index_in_dim)/dynamic_slice | solution.py:118
  127.0 3.1 %constant_dynamic-slice_fusion.5 = f32[1,2,64,10,64]{2,0,4,3,1:T(1,128)S(1)} fusion(f32[8,2,64,10,64]{2,0,4,3,1:T(8,128)} %get-tuple-element.235, s32[]{:T(128)} %get-tuple-element.219), kind=kLoop, calls=%fused_computation.37.clone.1 | loop fusion | bytes 655364 | tf_op jit(solution)/shard_map/while/body/jit(dynamic_index_in_dim)/dynamic_slice | solution.py:118
  134.2 2.3 reduce-window.6
  138.9 7.7 %all-gather.2 = f32[8,1,10]{2,1,0:T(1,128)S(1)} all-gather(f32[2,1,10]{2,1,0:T(1,128)S(1)} %get-tuple-element.140), channel_id=4, replica_groups=mesh['seq_0'=4,'seq_1'=4,'seq_2'=2,'tp'=8] {'seq_1'}, dimensions={0}, use_global_device_ids=true | all-gather | bytes 400 | tf_op jit(solution)/shard_map/all_gather | solution.py:35
  148.2 2.3 bitcast_add_fusion.4
  150.8 37.7 %all-gather.7.cloned.1.call-done = f32[4,2,10,64,128]{4,3,2,1,0:T(8,128)} async-done(((f32[1,2,10,64,128]{4,3,2,1,0:T(8,128)}), f32[4,2,10,64,128]{4,3,2,1,0:T(8,128)}) %all-gather.7.cloned.1.call-update) | async-done | bytes 2621456 | tf_op jit(solution)/shard_map/all_gather | solution.py:35
  188.5 2.8 %multiply_add_fusion.1 = f32[1,2,10,64,128]{4,3,2,1,0:T(8,128)} fusion(f32[4,2,10,64,128]{4,3,2,1,0:T(8,128)} %all-gather.7.cloned.1.call-done, f32[2,10]{1,0:T(2,128)S(1)} %get-tuple-element.144, f32[2,10]{1,0:T(2,128)S(1)} %bitcast.251, f32[2,10]{1,0:T(2,128)S(1)} %bitcast.248, f32[2,10]{1,0:T(2,128)S(1)} %bitcast.254), kind=kLoop, calls=%fused_computation.98 | loop fusion | flops 1146880 | bytes 3277120 | tf_op jit(solution)/shard_map/add | solution.py:77
  191.8 7.1 %fusion.36 = f32[1024,640]{1,0:T(8,128)S(1)} fusion(bf16[1024,2560]{1,0:T(8,128)(2,1)} %bitcast.230, bf16[2560,640]{1,0:T(8,128)(2,1)} %param.13), kind=kOutput, calls=%fused_computation.56 | convolution fusion | flops 3356753920 | bytes 11141120 | tf_op jit(solution)/shard_map/dot_general | solution.py:96
  199.0 2.3 copy.110
  201.3 4.8 %reshape.160 = f32[2,512,10,64]{1,0,3,2:T(2,128)} reshape(f32[1024,640]{0,1:T(8,128)} %copy.110) | data formatting | bytes 5242880 | tf_op jit(solution)/shard_map/convert_element_type | solution.py:143
  206.1 8.6 %all_gather.32 = f32[4,2,10]{2,1,0:T(2,128)S(1)} all-gather(f32[1,2,10]{2,1,0:T(2,128)S(1)} %bitcast.259), channel_id=1, replica_groups=mesh['seq_0'=4,'seq_1'=4,'seq_2'=2,'tp'=8] {'seq_0'}, dimensions={0}, use_global_device_ids=true | all-gather | bytes 400 | tf_op jit(solution)/shard_map/all_gather | solution.py:35
  214.6 9.2 %copy.102 = f32[2,8,64,10,64]{2,1,4,3,0:T(8,128)} copy(f32[2,8,64,10,64]{2,4,3,0,1:T(8,128)} %bitcast.237) | data formatting | bytes 5242880 | tf_op jit(solution)/shard_map/transpose | solution.py:129
  223.8 5.2 %reshape.155 = f32[2,512,10,64]{1,3,2,0:T(8,128)} reshape(f32[2,8,64,10,64]{2,1,4,3,0:T(8,128)} %copy.102) | data formatting | bytes 5242880 | tf_op jit(solution)/shard_map/reshape | solution.py:129
  229.3 9.1 %multiply_reduce_fusion = (f32[2,512]{1,0:T(2,128)S(1)}, f32[2,512,10,64]{1,3,2,0:T(8,128)}) fusion(f32[2,512,10,64]{1,0,3,2:T(2,128)S(1)} %copy-done.6, f32[2,512,10,64]{1,3,2,0:T(8,128)} %reshape.155, f32[2,512,10]{1,2,0:T(8,128)S(1)} %copy.108, f32[4,2,10,64,128]{4,3,2,1,0:T(8,128)} %all-gather.9.cloned.1.call-done, ...), kind=kOutput, calls=%fused_computation.51 | convolution fusion | flops 1017609216 | bytes 14988234 | tf_op jit(solution)/shard_map/btn,bhpn->bthp/dot_general | solution.py:139
  238.4 3.2 %copy.109 = f32[2,512,640]{2,1,0:T(8,128)} copy(f32[2,512,640]{1,2,0:T(8,128)} %bitcast.238) | data formatting | bytes 5242880 | tf_op jit(solution)/shard_map/reshape | solution.py:141
  241.6 13.7 %psum.7 = f32[2,512,1]{1,0,2:T(2,128)S(1)} all-reduce(f32[2,512,1]{1,0,2:T(2,128)S(1)} %bitcast.261), channel_id=1, replica_groups=mesh['seq_0'=4,'seq_1'=4,'seq_2'=2,'tp'=8] {'tp'}, use_global_device_ids=true, to_apply=%region_6.7 | all-reduce | flops 1024 | bytes 8192 | tf_op jit(solution)/shard_map/psum | solution.py:146
  255.4 4.6 %multiply_convert_fusion = bf16[2,512,640]{2,1,0:T(8,128)(2,1)} fusion(f32[2,512,640]{2,1,0:T(8,128)} %copy.109, f32[2,512,640]{2,1,0:T(8,128)} %bitcast.233, f32[640]{0:T(1024)S(1)} %copy-done.12, f32[2,512]{1,0:T(2,128)S(1)} %rsqrt_bitcast_fusion), kind=kLoop, calls=%fused_computation.50 | loop fusion | flops 5242880 | bytes 6560256 | tf_op jit(solution)/shard_map/convert_element_type | solution.py:147
  (203 shorter events, 50.7 us)
Async XLA Ops:
  6.5 1.9 copy-start
  6.5 141.7 %all-gather.11.cloned.1.call-start = ((), (), s32[]{:S(2)}) async-start(), calls=%async_computation.2 | async-start | bytes 1966080 | tf_op jit(solution)/shard_map/all_gather | solution.py:35
  8.5 6.2 %copy-start.3 = (bf16[2,512,2560]{2,1,0:T(8,128)(2,1)S(1)}, bf16[2,512,2560]{2,1,0:T(8,128)(2,1)}, u32[]{:S(2)}) copy-start(bf16[2,512,2560]{2,1,0:T(8,128)(2,1)} %param.12) | copy-start | bytes 15728644
  8.5 6.2 %copy-start.9 = (bf16[2560,32]{0,1:T(8,128)(2,1)S(1)}, bf16[2560,32]{0,1:T(8,128)(2,1)}, u32[]{:S(2)}) copy-start(bf16[2560,32]{0,1:T(8,128)(2,1)} %param.15) | copy-start | bytes 491524
  40.1 14.6 %copy-start.11 = (f32[4,640]{1,0:T(4,128)S(1)}, f32[4,640]{1,0:T(4,128)}, u32[]{:S(2)}) copy-start(f32[4,640]{1,0:T(4,128)} %param.17) | copy-start | bytes 30724
  40.1 14.6 %copy-start.15 = (f32[10]{0:T(128)S(1)}, f32[10]{0:T(128)}, u32[]{:S(2)}) copy-start(f32[10]{0:T(128)} %param.20) | copy-start | bytes 124
  40.1 14.6 %copy-start.10 = (bf16[2560,10]{0,1:T(8,128)(2,1)S(1)}, bf16[2560,10]{0,1:T(8,128)(2,1)}, u32[]{:S(2)}) copy-start(bf16[2560,10]{0,1:T(8,128)(2,1)} %param.16) | copy-start | bytes 153604
  40.1 14.6 %copy-start.14 = (f32[10]{0:T(128)S(1)}, f32[10]{0:T(128)}, u32[]{:S(2)}) copy-start(f32[10]{0:T(128)} %param.19) | copy-start | bytes 124
  44.6 14.2 %copy-start.13 = (f32[4,256]{1,0:T(4,128)S(1)}, f32[4,256]{1,0:T(4,128)}, u32[]{:S(2)}) copy-start(f32[4,256]{1,0:T(4,128)} %param.18) | copy-start | bytes 12292
  44.6 14.6 %collective-permute-start = (bf16[2,3,896]{2,1,0:T(4,128)(2,1)S(1)}, bf16[2,3,896]{2,1,0:T(4,128)(2,1)S(1)}, u32[]{:S(2)}, u32[]{:S(2)}) collective-permute-start(bf16[2,3,896]{2,1,0:T(4,128)(2,1)S(1)} %slice.155), channel_id=1, source_target_pairs={{0,8},{8,16},{16,24},{24,32},{32,40},{40,48},{48,56},{56,64},{64,7... | collective-permute-start | bytes 32264 | tf_op jit(solution)/shard_map/ppermute | solution.py:21
  61.7 2.2 copy-start.4
  66.2 4.9 %copy-start.7 = (f32[2,512,128]{2,1,0:T(8,128)S(1)}, f32[2,512,128]{2,1,0:T(8,128)}, u32[]{:S(2)}) copy-start(f32[2,512,128]{2,1,0:T(8,128)} %get-tuple-element.127) | copy-start | bytes 1572868
  66.2 4.9 %copy-start.8 = (f32[2,512,128]{2,1,0:T(8,128)S(1)}, f32[2,512,128]{2,1,0:T(8,128)}, u32[]{:S(2)}) copy-start(f32[2,512,128]{2,1,0:T(8,128)} %get-tuple-element.128) | copy-start | bytes 1572868
  133.3 0.8 copy-start.2
  134.1 54.4 %all-gather.7.cloned.1.call-start = ((), (), s32[]{:S(2)}) async-start(), calls=%async_computation | async-start | bytes 3276800 | tf_op jit(solution)/shard_map/all_gather | solution.py:35
  150.5 78.8 %all-gather.9.cloned.1.call-start = ((), (), s32[]{:S(2)}) async-start(), calls=%async_computation.1 | async-start | bytes 3276800 | tf_op jit(solution)/shard_map/all_gather | solution.py:35
  199.0 7.1 %copy-start.5 = (f32[1024,640]{1,0:T(8,128)}, f32[1024,640]{1,0:T(8,128)S(1)}, u32[]{:S(2)}) copy-start(f32[1024,640]{1,0:T(8,128)S(1)} %fusion.36) | copy-start | bytes 7864324
  223.8 5.5 %copy-start.6 = (f32[2,512,10,64]{1,0,3,2:T(2,128)S(1)}, f32[2,512,10,64]{1,0,3,2:T(2,128)}, u32[]{:S(2)}) copy-start(f32[2,512,10,64]{1,0,3,2:T(2,128)} %reshape.160) | copy-start | bytes 7864324
  238.4 17.0 %copy-start.12 = (f32[640]{0:T(1024)S(1)}, f32[640]{0:T(1024)}, u32[]{:S(2)}) copy-start(f32[640]{0:T(1024)} %param.21) | copy-start | bytes 7684
  255.3 4.7 %copy-start.1 = (bf16[2560,640]{1,0:T(8,128)(2,1)S(1)}, bf16[2560,640]{1,0:T(8,128)(2,1)}, u32[]{:S(2)}) copy-start(bf16[2560,640]{1,0:T(8,128)(2,1)} %param.14) | copy-start | bytes 9830404
Sparse Core Ops, SparseCore 0:
  134.3 13.8 all-gather.10
  150.6 37.8 all-gather.6
  191.4 37.7 all-gather.8
where the time goes:
time: 271 us; the launch traced here: 267 us
  local copies, waits for them, and re-layouts  69.9 us (26%)
  matrix products  59.8 us (22%)
  blocking collectives  55.5 us (20%)
  waiting for transfers between devices  39.6 us (15%)
  other arithmetic  17.2 us (6%)
  between operations  13.4 us (5%)
  starting transfers between devices  10.4 us (4%)
    all_gather x3, waiting for transfers between devices, entering(): pieces = jax.tree.map(lambda part: lax.all_gather(part, axis), so_far)  39.6 us
    dynamic_slice x32, local copies, waits for them, and re-layouts, on_device(): lax.scan(block_step, initial, (to_blocks(values, batch_size, blocks), to_...  26.5 us
    all_gather x1, blocking collectives, on_device(): bc_pre = lax.all_gather(bc_part, 'tp', axis=1, tiled=True)  23.7 us
    all_gather x3, blocking collectives, entering(): pieces = jax.tree.map(lambda part: lax.all_gather(part, axis), so_far)  18.1 us
    dot_general x8, matrix products, block_step(): jnp.einsum('bijh,bjhp->bihp', mixing, values, precision=lax.Precision.HIG...  17.6 us
    psum x1, blocking collectives, on_device(): whole_sq = lax.psum(squares, 'tp')  13.7 us
    ppermute x1, starting transfers between devices, passed_along(): return lax.ppermute(block, axis, route)  10.1 us
    transpose x1, local copies, waits for them, and re-layouts, on_device(): jnp.moveaxis(outputs, 0, 1)  9.16 us
  transfers between devices with their start and end apart: 4, of which 3 were waited for; matrix products, arithmetic and copies ran while one was open for 14% of the time, Pallas kernels for 0%

commit v1 on v0

v1 whole, which is shorter than its diff:
```python
import functools
import math

import jax
import jax.numpy as jnp
from jax import lax
from jax.experimental import pallas as pl
from jax.experimental.pallas import tpu as pltpu
from jax.sharding import PartitionSpec as P

MESH = pl.DeviceIdType.MESH
F32, BF16 = jnp.float32, jnp.bfloat16
HEAD_DIM = 64
STATE = 128
CONV = 4
HALO = 16
CHUNK = 128
EPSILON = 1e-05
NN = (((1,), (0,)), ((), ()))
TN = (((0,), (0,)), ((), ()))
NT = (((1,), (1,)), ((), ()))


def dot(a, b, dims=NN):
    return lax.dot_general(a, b, dims, preferred_element_type=F32)


def split2(x):
    high = x.astype(BF16)
    low = (x - high.astype(F32)).astype(BF16)
    return jnp.concatenate([high, low], axis=0)


def silu(x):
    return x * lax.logistic(x)


def conv_silu(window, taps, rows):
    total = taps[0:1] * window[5 : 5 + rows]
    for k in range(1, CONV):
        total = total + taps[k : k + 1] * window[5 + k : 5 + k + rows]
    return silu(total)


def kernel(
    n, nz, batch, length, inner, heads,
    hid_in, gate_in, value_in, bc_in, step_in, vconv, bconv, bias, rate, gain,
    out,
    hid, wcat, bcw, stw, wsm, small, pre, xp, lhs, tbuf, bct, bcall, dsend, dall, dexp,
    sbuf, rbuf, pbuf, qbuf, sssend, ssall, rowx, e1t, e2t,
    load_sem, halo_s, halo_r, bc_s, bc_r, d_s, d_r, p_s, p_r, q_s, q_r, ss_s, ss_r,
):
    me = lax.axis_index("seq")
    z = lax.axis_index("tp")
    step_rows = length + HALO
    chunks = length // CHUNK
    piece = batch * STATE // n
    per_batch = n // batch
    nbc = bct.shape[0]
    width = hid.shape[1]

    loads = []
    for b in range(batch):
        loads.append(
            pltpu.make_async_copy(
                hid_in.at[b], hid.at[pl.ds(b * step_rows + HALO, length)], load_sem.at[b]
            )
        )
    loads.append(pltpu.make_async_copy(bc_in, bcw, load_sem.at[2]))
    loads.append(pltpu.make_async_copy(step_in, stw, load_sem.at[3]))
    loads.append(pltpu.make_async_copy(value_in, wcat.at[:, pl.ds(0, inner)], load_sem.at[4]))
    loads.append(pltpu.make_async_copy(gate_in, wcat.at[:, pl.ds(inner, inner)], load_sem.at[5]))
    for k in (2, 3, 0, 1, 4, 5):
        loads[k].start()

    barrier = pltpu.get_barrier_semaphore()

    def greet_seq(d, carry):
        pl.semaphore_signal(
            barrier, inc=1, device_id={"seq": lax.rem(me + d, n)}, device_id_type=MESH
        )
        return carry

    def greet_tp(d, carry):
        pl.semaphore_signal(
            barrier, inc=1, device_id={"tp": lax.rem(z + d, nz)}, device_id_type=MESH
        )
        return carry

    lax.fori_loop(1, n, greet_seq, 0)
    lax.fori_loop(1, nz, greet_tp, 0)

    head_of = lax.broadcasted_iota(jnp.int32, (16, inner), 1) // HEAD_DIM
    spread16 = (head_of == lax.broadcasted_iota(jnp.int32, (16, inner), 0)).astype(F32)
    spread = jnp.concatenate([spread16, spread16], axis=0).astype(BF16)
    upper = (
        lax.broadcasted_iota(jnp.int32, (length, length), 0)
        <= lax.broadcasted_iota(jnp.int32, (length, length), 1)
    ).astype(F32).astype(BF16)

    pl.semaphore_wait(barrier, n - 1 + nz - 1)

    def halo_copy(b, target):
        return pltpu.make_async_remote_copy(
            src_ref=hid_in.at[b, pl.ds(length - HALO, HALO)],
            dst_ref=hid.at[pl.ds(b * step_rows, HALO)],
            send_sem=halo_s.at[b],
            recv_sem=halo_r.at[b],
            device_id={"seq": target},
            device_id_type=MESH,
        )

    following = lax.rem(me + 1, n)

    @pl.when(me < n - 1)
    def _():
        for b in range(batch):
            halo_copy(b, following).start()

    @pl.when(me == 0)
    def _():
        for b in range(batch):
            hid[pl.ds(b * step_rows, HALO), :] = jnp.zeros((HALO, width), BF16)

    loads[2].wait()
    loads[3].wait()
    wsm[:, 0:nbc] = bcw[...]
    wsm[:, 128 : 128 + heads] = stw[...]
    for b in range(batch):
        loads[b].wait()
        rows = pl.ds(b * step_rows + HALO, length)
        small[rows, :] = dot(hid[rows, :], wsm[...])

    @pl.when(me > 0)
    def _():
        for b in range(batch):
            halo_copy(b, following).wait_recv()

    edge = dot(
        jnp.concatenate([hid[pl.ds(b * step_rows, HALO), :] for b in range(batch)], axis=0),
        wsm[...],
    )
    for b in range(batch):
        small[pl.ds(b * step_rows, HALO), :] = edge[b * HALO : (b + 1) * HALO]

    taps = pltpu.roll(
        jnp.concatenate([bconv[...], jnp.zeros((8 - CONV, 2 * STATE), F32)], axis=0),
        lax.rem(2 * STATE - z * nbc, 2 * STATE),
        1,
    )[:, 0:128]
    for b in range(batch):
        base = b * step_rows
        window = small[pl.ds(base + 8, length + 8), 0:128].astype(BF16).astype(F32)
        rows = conv_silu(window, taps, length)
        bct[:, b * length : (b + 1) * length] = jnp.transpose(rows)[0:nbc].astype(BF16)
    bcall[z] = bct[...]

    def bc_copy(source, target):
        return pltpu.make_async_remote_copy(
            src_ref=bct,
            dst_ref=bcall.at[source],
            send_sem=bc_s.at[target],
            recv_sem=bc_r.at[source],
            device_id={"tp": target},
            device_id_type=MESH,
        )

    def bc_start(d, carry):
        bc_copy(z, lax.rem(z + d, nz)).start()
        return carry

    lax.fori_loop(1, nz, bc_start, 0)

    table = jnp.concatenate([bias[...], rate[...], jnp.zeros((6, heads), F32)], axis=0)
    table = jnp.concatenate([table, jnp.zeros((8, 128 - heads), F32)], axis=1)
    columns = jnp.transpose(table)
    bias_col, rate_col = columns[0:16, 0:1], jnp.exp(columns[0:16, 1:2])
    live = lax.broadcasted_iota(jnp.int32, (16, length), 0) < heads
    steps, parts = [], []
    for b in range(batch):
        raw = jnp.transpose(small[pl.ds(b * step_rows + HALO, length), 128:256])[0:16]
        raw = jnp.where(live, raw + bias_col, 0.0)
        size = jnp.maximum(raw, 0.0) + jnp.log1p(jnp.exp(-jnp.abs(raw)))
        size = jnp.where(live, size, 0.0)
        steps.append(size)
        parts.append(split2(-size * rate_col))
    summed = dot(jnp.concatenate(parts, axis=0), upper)
    lane = lax.broadcasted_iota(jnp.int32, (16, 128), 1)
    factors = jnp.zeros((16, 128), F32)
    for b in range(batch):
        cum = summed[32 * b : 32 * b + 16] + summed[32 * b + 16 : 32 * b + 32]
        begin = jnp.zeros((16, 1), F32)
        for c in range(chunks):
            here = cum[:, c * CHUNK : (c + 1) * CHUNK]
            end = here[:, CHUNK - 1 : CHUNK]
            ref = 0.5 * (begin + end)
            q = b * chunks + c
            e1t[q] = split2(jnp.exp(ref - here) * steps[b][:, c * CHUNK : (c + 1) * CHUNK])
            e2t[q] = split2(jnp.exp(here - ref))
            for kind, value in enumerate((ref - begin, end - begin, end - ref, ref)):
                factors = jnp.where(lane == kind * 8 + q, value, factors)
            begin = end
        factors = jnp.where(lane == 32 + b, begin, factors)
    factors = jnp.exp(factors)
    rowx[...] = dot(split2(factors), spread, TN)
    totals = jnp.transpose(factors)
    for b in range(batch):
        row = jnp.concatenate(
            [totals[32 + b : 33 + b], jnp.zeros((1, 112), F32)], axis=1
        )
        dsend[b] = jnp.broadcast_to(row, (8, 128))

    def d_copy(source, target):
        return pltpu.make_async_remote_copy(
            src_ref=dsend.at[target // per_batch],
            dst_ref=dall.at[source],
            send_sem=d_s.at[target],
            recv_sem=d_r.at[source],
            device_id={"seq": target},
            device_id_type=MESH,
        )

    def d_start(d, carry):
        d_copy(me, lax.rem(me + d, n)).start()
        return carry

    lax.fori_loop(1, n, d_start, 0)
    dall[me] = dsend[me // per_batch]

    loads[4].wait()
    loads[5].wait()

    def project(t, carry):
        columns_at = pl.ds(pl.multiple_of(t * 256, 256), 256)
        for half in range(batch):
            rows = pl.ds(half * step_rows, step_rows)
            pre[rows, columns_at] = (
                dot(hid[rows, :], wcat[:, columns_at]).astype(BF16).astype(F32)
            )
        return carry

    lax.fori_loop(0, 2 * inner // 256, project, 0)

    vtaps = vconv[...]

    def values_of(q, carry):
        base = pl.multiple_of((q // chunks) * step_rows + lax.rem(q, chunks) * CHUNK + 8, 8)
        rows = conv_silu(pre[pl.ds(base, CHUNK + 8), 0:inner], vtaps, CHUNK)
        xp[q] = (rows * dot(e1t[q], spread, TN)).astype(BF16)
        at = pl.ds(base + 8, CHUNK)
        pre[at, inner:] = silu(pre[at, inner:]) * dot(e2t[q], spread, TN)
        return carry

    lax.fori_loop(0, batch * chunks, values_of, 0)

    def bc_wait(d, carry):
        bc_copy(lax.rem(z + d, nz), z).wait_recv()
        return carry

    lax.fori_loop(1, nz, bc_wait, 0)
    half = nz // 2
    causal = (
        lax.broadcasted_iota(jnp.int32, (CHUNK, CHUNK), 0)
        >= lax.broadcasted_iota(jnp.int32, (CHUNK, CHUNK), 1)
    )
    for b in range(batch):
        state = jnp.zeros((STATE, inner), F32)
        for c in range(chunks):
            q = b * chunks + c
            lanes = slice(b * length + c * CHUNK, b * length + (c + 1) * CHUNK)
            rows = bcall[0:half, :, lanes].reshape(STATE, CHUNK)
            if c:
                tbuf[q] = state * rowx[q : q + 1]
                state = state * rowx[8 + q : 9 + q]
            else:
                tbuf[q] = jnp.zeros((STATE, inner), F32)
            state = state + rowx[16 + q : 17 + q] * dot(rows, xp[q])
        sbuf[b * per_batch : (b + 1) * per_batch] = state.reshape(
            per_batch, piece, inner
        ).astype(BF16)
    rbuf[me] = sbuf[me]

    def p_copy(source, target):
        return pltpu.make_async_remote_copy(
            src_ref=sbuf.at[target],
            dst_ref=rbuf.at[source],
            send_sem=p_s.at[target],
            recv_sem=p_r.at[source],
            device_id={"seq": target},
            device_id_type=MESH,
        )

    def p_start(d, carry):
        p_copy(me, lax.rem(me + d, n)).start()
        return carry

    lax.fori_loop(1, n, p_start, 0)

    def d_wait(d, carry):
        d_copy(lax.rem(me + d, n), me).wait_recv()
        return carry

    lax.fori_loop(1, n, d_wait, 0)
    decays = dall[...].reshape(n * 8, 128)[:, 0:16]
    high = decays.astype(BF16)
    low = (decays - high.astype(F32)).astype(BF16)
    dexp[...] = (dot(high, spread[0:16]) + dot(low, spread[0:16])).reshape(n, 8, inner)

    for q in range(batch * chunks):
        lanes = slice(q * CHUNK, (q + 1) * CHUNK)
        b_t = bcall[0:half, :, lanes].reshape(STATE, CHUNK)
        c_t = bcall[half:nz, :, lanes].reshape(STATE, CHUNK)
        scores = dot(c_t, b_t, TN)
        lhs[q, :, 0:CHUNK] = jnp.where(causal, scores, 0.0).astype(BF16)
        lhs[q, :, CHUNK:] = jnp.transpose(c_t.astype(F32)).astype(BF16)

    def scan_step(i, prefix):
        @pl.when(i != me)
        def _():
            p_copy(i, me).wait_recv()

        pbuf[i] = prefix.astype(BF16)
        return dexp[i, 0:1, :] * prefix + rbuf[i].astype(F32)

    lax.fori_loop(0, n, scan_step, jnp.zeros((piece, inner), F32))

    def q_copy(source, target):
        return pltpu.make_async_remote_copy(
            src_ref=pbuf.at[target],
            dst_ref=qbuf.at[source],
            send_sem=q_s.at[target],
            recv_sem=q_r.at[source],
            device_id={"seq": target},
            device_id_type=MESH,
        )

    def q_start(d, carry):
        q_copy(me, lax.rem(me + d, n)).start()
        return carry

    lax.fori_loop(1, n, q_start, 0)
    qbuf[me] = pbuf[me]

    def q_wait(d, carry):
        q_copy(lax.rem(me + d, n), me).wait_recv()
        return carry

    lax.fori_loop(1, n, q_wait, 0)

    ones = jnp.ones((8, inner), BF16)
    picked = lax.broadcasted_iota(jnp.int32, (8, CHUNK), 0)
    squares = jnp.zeros((8, CHUNK), F32)
    gains = gain[...]
    for b in range(batch):
        entering = qbuf[b * per_batch : (b + 1) * per_batch].astype(F32).reshape(STATE, inner)
        for c in range(chunks):
            q = b * chunks + c
            state = (tbuf[q] + entering * rowx[24 + q : 25 + q]).astype(BF16)
            at = pl.ds(b * step_rows + HALO + c * CHUNK, CHUNK)
            mixed = dot(lhs[q], jnp.concatenate([xp[q], state], axis=0))
            gated = mixed * pre[at, inner:]
            pre[at, 0:inner] = gated * gains
            sums = dot(ones, (gated * gated).astype(BF16), NT)
            squares = jnp.where(picked == q, sums, squares)
    sssend[...] = squares

    def ss_copy(source, target):
        return pltpu.make_async_remote_copy(
            src_ref=sssend,
            dst_ref=ssall.at[source],
            send_sem=ss_s.at[target],
            recv_sem=ss_r.at[source],
            device_id={"tp": target},
            device_id_type=MESH,
        )

    def ss_start(d, carry):
        ss_copy(z, lax.rem(z + d, nz)).start()
        return carry

    lax.fori_loop(1, nz, ss_start, 0)
    ssall[z] = squares

    def ss_wait(d, carry):
        ss_copy(lax.rem(z + d, nz), z).wait_recv()
        return carry

    lax.fori_loop(1, nz, ss_wait, 0)
    whole = ssall[0]
    for s in range(1, nz):
        whole = whole + ssall[s]
    factor = lax.rsqrt(whole / (inner * nz) + EPSILON)
    wide = jnp.ones((16, 128), BF16)
    for b in range(batch):
        for c in range(chunks):
            q = b * chunks + c
            mine = split2(jnp.where(picked == q, factor, 0.0))
            scale = dot(mine, wide, TN)
            at = pl.ds(b * step_rows + HALO + c * CHUNK, CHUNK)
            for col in range(0, inner, 128):
                out[b, c * CHUNK : (c + 1) * CHUNK, col : col + 128] = (
                    pre[at, col : col + 128] * scale
                ).astype(BF16)

    @pl.when(me < n - 1)
    def _():
        for b in range(batch):
            halo_copy(b, following).wait_send()

    def seq_sent(d, carry):
        other = lax.rem(me + d, n)
        d_copy(me, other).wait_send()
        p_copy(me, other).wait_send()
        q_copy(me, other).wait_send()
        return carry

    def tp_sent(d, carry):
        other = lax.rem(z + d, nz)
        bc_copy(z, other).wait_send()
        ss_copy(z, other).wait_send()
        return carry

    lax.fori_loop(1, n, seq_sent, 0)
    lax.fori_loop(1, nz, tp_sent, 0)


def on_device(
    n, nz, hidden_in, gate_proj, value_proj, bc_proj, step_proj,
    value_conv, bc_conv, step_bias, log_rate, norm_gain,
):
    batch, length, width = hidden_in.shape
    inner, heads, nbc = value_proj.shape[1], step_proj.shape[1], bc_proj.shape[1]
    chunks = batch * length // CHUNK
    rows = batch * (length + HALO)
    piece = batch * STATE // n
    hbm = pl.BlockSpec(memory_space=pl.ANY)
    vmem = pl.BlockSpec(memory_space=pltpu.VMEM)
    dma = pltpu.SemaphoreType.DMA
    return pl.pallas_call(
        functools.partial(kernel, n, nz, batch, length, inner, heads),
        out_shape=jax.ShapeDtypeStruct((batch, length, inner), BF16),
        in_specs=[hbm] * 5 + [vmem] * 5,
        out_specs=vmem,
        scratch_shapes=[
            pltpu.VMEM((rows, width), BF16),
            pltpu.VMEM((width, 2 * inner), BF16),
            pltpu.VMEM((width, nbc), BF16),
            pltpu.VMEM((width, heads), BF16),
            pltpu.VMEM((width, 256), BF16),
            pltpu.VMEM((rows, 256), F32),
            pltpu.VMEM((rows, 2 * inner), F32),
            pltpu.VMEM((chunks, CHUNK, inner), BF16),
            pltpu.VMEM((chunks, CHUNK, CHUNK + STATE), BF16),
            pltpu.VMEM((chunks, STATE, inner), F32),
            pltpu.VMEM((nbc, batch * length), BF16),
            pltpu.VMEM((nz, nbc, batch * length), BF16),
            pltpu.VMEM((batch, 8, 128), F32),
            pltpu.VMEM((n, 8, 128), F32),
            pltpu.VMEM((n, 8, inner), F32),
            pltpu.VMEM((n, piece, inner), BF16),
            pltpu.VMEM((n, piece, inner), BF16),
            pltpu.VMEM((n, piece, inner), BF16),
            pltpu.VMEM((n, piece, inner), BF16),
            pltpu.VMEM((8, CHUNK), F32),
            pltpu.VMEM((nz, 8, CHUNK), F32),
            pltpu.VMEM((128, inner), F32),
            pltpu.VMEM((chunks, 32, CHUNK), BF16),
            pltpu.VMEM((chunks, 32, CHUNK), BF16),
            dma((6,)),
            dma((batch,)), dma((batch,)),
            dma((nz,)), dma((nz,)),
            dma((n,)), dma((n,)),
            dma((n,)), dma((n,)),
            dma((n,)), dma((n,)),
            dma((nz,)), dma((nz,)),
        ],
        compiler_params=pltpu.CompilerParams(
            collective_id=0, has_side_effects=True, vmem_limit_bytes=60 * 1024 * 1024
        ),
    )(
        hidden_in, gate_proj, value_proj, bc_proj, step_proj, value_conv, bc_conv,
        step_bias.reshape(1, heads), log_rate.reshape(1, heads), norm_gain.reshape(1, inner),
    )


def solution(mesh):
    n, nz = mesh.shape["seq"], mesh.shape["tp"]
    return jax.shard_map(
        functools.partial(on_device, n, nz),
        mesh=mesh,
        in_specs=(
            P(None, "seq", None), P(None, "tp"), P(None, "tp"), P(None, "tp"), P(None, "tp"),
            P(None, "tp"), P(), P("tp"), P("tp"), P("tp"),
        ),
        out_specs=P(None, "seq", "tp"),
        check_vma=False,
    )
```

time: 271 us -> 60.5 us (0.22); the launches traced: 267 us -> 60.2 us
  local copies, waits for them, and re-layouts: 69.9 us -> 7.8 us
  matrix products: 59.8 us -> 0 us
  blocking collectives: 55.5 us -> 0 us
  Pallas kernels: 0 us -> 52.4 us
  waiting for transfers between devices: 39.6 us -> 0 us
  other arithmetic: 17.2 us -> 0 us
  between operations: 13.4 us -> 0.01 us
  starting transfers between devices: 10.4 us -> 0 us
    dot_general x37 -> x0, matrix products: 59.8 us -> none  [the longest x8 17.6 us: block_step(): jnp.einsum('bijh,bjhp->bihp', mixing, values, precision=lax.Precision.HIG...]
    pallas_call x0 -> x1, Pallas kernels: none -> 52.4 us  [on_device(): pl.pallas_call(functools.partial(kernel, n, nz, batch, length, inner, hea...]
    all_gather x4 -> x0, blocking collectives: 41.8 us -> none  [the longest x1 23.7 us: on_device(): bc_pre = lax.all_gather(bc_part, 'tp', axis=1, tiled=True)]
    all_gather x3 -> x0, waiting for transfers between devices: 39.6 us -> none  [entering(): pieces = jax.tree.map(lambda part: lax.all_gather(part, axis), so_far)]
    dynamic_slice x32 -> x0, local copies, waits for them, and re-layouts: 26.5 us -> none  [on_device(): lax.scan(block_step, initial, (to_blocks(values, batch_size, blocks), to_...]
    psum x1 -> x0, blocking collectives: 13.7 us -> none  [on_device(): whole_sq = lax.psum(squares, 'tp')]
    reshape x7 -> x1, local copies, waits for them, and re-layouts: 11.7 us -> 1.28 us  [on_device(): norm_gain.reshape(1, inner)]
    ppermute x1 -> x0, starting transfers between devices: 10.1 us -> none  [passed_along(): return lax.ppermute(block, axis, route)]
  transfers between devices with their start and end apart: 4 -> 0, of which waited for: 3 -> 0; matrix products, arithmetic and copies ran while one was open for 14% -> 0% of each run, Pallas kernels for 0% -> 0%
where the time goes in v1:
time: 60.5 us; the launch traced here: 60.2 us
  Pallas kernels  52.4 us (87%)
  local copies, waits for them, and re-layouts  7.8 us (13%)
    pallas_call x1, Pallas kernels, on_device(): pl.pallas_call(functools.partial(kernel, n, nz, batch, length, inner, hea...  52.4 us
    unnamed x3, local copies, waits for them, and re-layouts  6.52 us
    reshape x1, local copies, waits for them, and re-layouts, on_device(): norm_gain.reshape(1, inner)  1.28 us

profile of v1, /device:TPU:1, one launch (start us, length us, event | category | flops | bytes accessed | tf_op | source)
XLA Modules:
  0.0 60.2 jit_solution(14738336442339861694)
XLA Ops:
  0.0 1.3 %reshape.11.gain = f32[1,640]{1,0:T(1,128)} reshape(f32[640]{0:T(1024)} %param.19) | data formatting | bytes 5120 | tf_op jit(solution)/shard_map/reshape | solution.py:482
  1.3 2.0 %copy.11.bc_in = bf16[2560,32]{1,0:T(8,128)(2,1)} copy(bf16[2560,32]{0,1:T(8,128)(2,1)} %param.13) | data formatting | bytes 327680 | tf_op args[3]
  3.3 2.0 %copy.12.step_in = bf16[2560,10]{1,0:T(8,128)(2,1)} copy(bf16[2560,10]{0,1:T(8,128)(2,1)} %param.14) | data formatting | bytes 102400 | tf_op args[4]
  5.3 52.4 %shard_map.100 = bf16[2,512,640]{2,1,0:T(8,128)(2,1)} custom-call(bf16[2,512,2560]{2,1,0:T(8,128)(2,1)} %hid_in.1, bf16[2560,640]{1,0:T(8,128)(2,1)} %gate_in.1, bf16[2560,640]{1,0:T(8,128)(2,1)} %value_in.1, bf16[2560,32]{1,0:T(8,128)(2,1)} %copy.11.bc_in, bf16[2560,10]{1,0:T(8,128)(2,1)} %copy.12.step_in, f32[4,640]{1,0:T(4,128)} %vconv.1, ...), custom_call_target="tpu_custom_call" | custom-call | tf_op jit(solution)/shard_map/pallas_call | solution.py:439
  57.8 2.5 %copy.14 = bf16[2,512,640]{2,1,0:T(8,128)(2,1)} copy(bf16[2,512,640]{2,1,0:T(8,128)(2,1)} %shard_map.100) | data formatting | bytes 2621440

commit v2 on v1

--- a/solution.py
+++ b/solution.py
@@ -32,7 +32,8 @@
 
 
 def silu(x):
-    return x * lax.logistic(x)
+    half = 0.5 * x
+    return half * jnp.tanh(half) + half
 
 
 def conv_silu(window, taps, rows):
@@ -44,9 +45,9 @@
 
 def kernel(
     n, nz, batch, length, inner, heads,
-    hid_in, gate_in, value_in, bc_in, step_in, vconv, bconv, bias, rate, gain,
+    hid_in, gate_in, value_in, bc_in, step_in, vconv_in, bconv_in, bias_in, rate_in, gain_in,
     out,
-    hid, wcat, bcw, stw, wsm, small, pre, xp, lhs, tbuf, bct, bcall, dsend, dall, dexp,
+    vconv, bconv, bias, rate, gain, hid, wcat, stw, wsm, small, pre, xp, lhs, tbuf, bct, bcall, dsend, dall, dexp,
     sbuf, rbuf, pbuf, qbuf, sssend, ssall, rowx, e1t, e2t,
     load_sem, halo_s, halo_r, bc_s, bc_r, d_s, d_r, p_s, p_r, q_s, q_r, ss_s, ss_r,
 ):
@@ -66,11 +67,14 @@
                 hid_in.at[b], hid.at[pl.ds(b * step_rows + HALO, length)], load_sem.at[b]
             )
         )
-    loads.append(pltpu.make_async_copy(bc_in, bcw, load_sem.at[2]))
+    loads.append(pltpu.make_async_copy(bc_in, wsm.at[pl.ds(0, nbc)], load_sem.at[2]))
     loads.append(pltpu.make_async_copy(step_in, stw, load_sem.at[3]))
     loads.append(pltpu.make_async_copy(value_in, wcat.at[:, pl.ds(0, inner)], load_sem.at[4]))
     loads.append(pltpu.make_async_copy(gate_in, wcat.at[:, pl.ds(inner, inner)], load_sem.at[5]))
-    for k in (2, 3, 0, 1, 4, 5):
+    tables = ((vconv_in, vconv), (bconv_in, bconv), (bias_in, bias), (rate_in, rate), (gain_in, gain))
+    for k, (source, target) in enumerate(tables):
+        loads.append(pltpu.make_async_copy(source, target, load_sem.at[6 + k]))
+    for k in (2, 3, 0, 1, 8, 9, 7, 6, 10, 4, 5):
         loads[k].start()
 
     barrier = pltpu.get_barrier_semaphore()
@@ -98,6 +102,17 @@
         <= lax.broadcasted_iota(jnp.int32, (length, length), 1)
     ).astype(F32).astype(BF16)
 
+    loads[2].wait()
+    loads[3].wait()
+    wsm[nbc : nbc + heads, :] = stw[...]
+    wsm[nbc + heads : nbc + 16, :] = jnp.zeros((16 - heads, width), BF16)
+
+    def project_small(b):
+        loads[b].wait()
+        rows = pl.ds(b * step_rows + HALO, length)
+        small[rows, :] = dot(hid[rows, :], wsm[...], NT)
+
+    project_small(0)
     pl.semaphore_wait(barrier, n - 1 + nz - 1)
 
     def halo_copy(b, target):
@@ -122,55 +137,11 @@
         for b in range(batch):
             hid[pl.ds(b * step_rows, HALO), :] = jnp.zeros((HALO, width), BF16)
 
-    loads[2].wait()
-    loads[3].wait()
-    wsm[:, 0:nbc] = bcw[...]
-    wsm[:, 128 : 128 + heads] = stw[...]
-    for b in range(batch):
-        loads[b].wait()
-        rows = pl.ds(b * step_rows + HALO, length)
-        small[rows, :] = dot(hid[rows, :], wsm[...])
-
-    @pl.when(me > 0)
-    def _():
-        for b in range(batch):
-            halo_copy(b, following).wait_recv()
-
-    edge = dot(
-        jnp.concatenate([hid[pl.ds(b * step_rows, HALO), :] for b in range(batch)], axis=0),
-        wsm[...],
-    )
-    for b in range(batch):
-        small[pl.ds(b * step_rows, HALO), :] = edge[b * HALO : (b + 1) * HALO]
-
-    taps = pltpu.roll(
-        jnp.concatenate([bconv[...], jnp.zeros((8 - CONV, 2 * STATE), F32)], axis=0),
-        lax.rem(2 * STATE - z * nbc, 2 * STATE),
-        1,
-    )[:, 0:128]
-    for b in range(batch):
-        base = b * step_rows
-        window = small[pl.ds(base + 8, length + 8), 0:128].astype(BF16).astype(F32)
-        rows = conv_silu(window, taps, length)
-        bct[:, b * length : (b + 1) * length] = jnp.transpose(rows)[0:nbc].astype(BF16)
-    bcall[z] = bct[...]
-
-    def bc_copy(source, target):
-        return pltpu.make_async_remote_copy(
-            src_ref=bct,
-            dst_ref=bcall.at[source],
-            send_sem=bc_s.at[target],
-            recv_sem=bc_r.at[source],
-            device_id={"tp": target},
-            device_id_type=MESH,
-        )
-
-    def bc_start(d, carry):
-        bc_copy(z, lax.rem(z + d, nz)).start()
-        return carry
-
-    lax.fori_loop(1, nz, bc_start, 0)
-
+    for b in range(1, batch):
+        project_small(b)
+
+    loads[8].wait()
+    loads[9].wait()
     table = jnp.concatenate([bias[...], rate[...], jnp.zeros((6, heads), F32)], axis=0)
     table = jnp.concatenate([table, jnp.zeros((8, 128 - heads), F32)], axis=1)
     columns = jnp.transpose(table)
@@ -178,7 +149,7 @@
     live = lax.broadcasted_iota(jnp.int32, (16, length), 0) < heads
     steps, parts = [], []
     for b in range(batch):
-        raw = jnp.transpose(small[pl.ds(b * step_rows + HALO, length), 128:256])[0:16]
+        raw = jnp.transpose(small[pl.ds(b * step_rows + HALO, length), nbc : nbc + 16])
         raw = jnp.where(live, raw + bias_col, 0.0)
         size = jnp.maximum(raw, 0.0) + jnp.log1p(jnp.exp(-jnp.abs(raw)))
         size = jnp.where(live, size, 0.0)
@@ -227,6 +198,49 @@
     lax.fori_loop(1, n, d_start, 0)
     dall[me] = dsend[me // per_batch]
 
+    @pl.when(me > 0)
+    def _():
+        for b in range(batch):
+            halo_copy(b, following).wait_recv()
+
+    edge = dot(
+        jnp.concatenate([hid[pl.ds(b * step_rows, HALO), :] for b in range(batch)], axis=0),
+        wsm[...],
+        NT,
+    )
+    for b in range(batch):
+        small[pl.ds(b * step_rows, HALO), :] = edge[b * HALO : (b + 1) * HALO]
+
+    loads[7].wait()
+    taps = pltpu.roll(
+        jnp.concatenate([bconv[...], jnp.zeros((8 - CONV, 2 * STATE), F32)], axis=0),
+        lax.rem(2 * STATE - z * nbc, 2 * STATE),
+        1,
+    )[:, 0:nbc]
+    for b in range(batch):
+        base = b * step_rows
+        window = small[pl.ds(base + 8, length + 8), 0:nbc].astype(BF16).astype(F32)
+        rows = conv_silu(window, taps, length)
+        bct[:, b * length : (b + 1) * length] = jnp.transpose(rows).astype(BF16)
+    bcall[z] = bct[...]
+
+    def bc_copy(source, target):
+        return pltpu.make_async_remote_copy(
+            src_ref=bct,
+            dst_ref=bcall.at[source],
+            send_sem=bc_s.at[target],
+            recv_sem=bc_r.at[source],
+            device_id={"tp": target},
+            device_id_type=MESH,
+        )
+
+    def bc_start(d, carry):
+        bc_copy(z, lax.rem(z + d, nz)).start()
+        return carry
+
+    half = nz // 2
+    lax.fori_loop(1, nz, bc_start, 0)
+
     loads[4].wait()
     loads[5].wait()
 
@@ -239,26 +253,39 @@
             )
         return carry
 
-    lax.fori_loop(0, 2 * inner // 256, project, 0)
-
+    value_tiles = -(-inner // 256)
+    lax.fori_loop(0, value_tiles, project, 0)
+
+    loads[6].wait()
     vtaps = vconv[...]
 
     def values_of(q, carry):
         base = pl.multiple_of((q // chunks) * step_rows + lax.rem(q, chunks) * CHUNK + 8, 8)
         rows = conv_silu(pre[pl.ds(base, CHUNK + 8), 0:inner], vtaps, CHUNK)
         xp[q] = (rows * dot(e1t[q], spread, TN)).astype(BF16)
-        at = pl.ds(base + 8, CHUNK)
+        return carry
+
+    lax.fori_loop(0, batch * chunks, values_of, 0)
+
+    lax.fori_loop(value_tiles, 2 * inner // 256, project, 0)
+
+    def gates_of(q, carry):
+        base = pl.multiple_of((q // chunks) * step_rows + lax.rem(q, chunks) * CHUNK + HALO, 8)
+        at = pl.ds(base, CHUNK)
         pre[at, inner:] = silu(pre[at, inner:]) * dot(e2t[q], spread, TN)
         return carry
 
-    lax.fori_loop(0, batch * chunks, values_of, 0)
-
-    def bc_wait(d, carry):
-        bc_copy(lax.rem(z + d, nz), z).wait_recv()
-        return carry
-
-    lax.fori_loop(1, nz, bc_wait, 0)
-    half = nz // 2
+    lax.fori_loop(0, batch * chunks, gates_of, 0)
+
+    def bc_wait(s, carry):
+        @pl.when(s != z)
+        def _():
+            bc_copy(s, z).wait_recv()
+
+        return carry
+
+    lax.fori_loop(0, half, bc_wait, 0)
+
     causal = (
         lax.broadcasted_iota(jnp.int32, (CHUNK, CHUNK), 0)
         >= lax.broadcasted_iota(jnp.int32, (CHUNK, CHUNK), 1)
@@ -306,14 +333,6 @@
     low = (decays - high.astype(F32)).astype(BF16)
     dexp[...] = (dot(high, spread[0:16]) + dot(low, spread[0:16])).reshape(n, 8, inner)
 
-    for q in range(batch * chunks):
-        lanes = slice(q * CHUNK, (q + 1) * CHUNK)
-        b_t = bcall[0:half, :, lanes].reshape(STATE, CHUNK)
-        c_t = bcall[half:nz, :, lanes].reshape(STATE, CHUNK)
-        scores = dot(c_t, b_t, TN)
-        lhs[q, :, 0:CHUNK] = jnp.where(causal, scores, 0.0).astype(BF16)
-        lhs[q, :, CHUNK:] = jnp.transpose(c_t.astype(F32)).astype(BF16)
-
     def scan_step(i, prefix):
         @pl.when(i != me)
         def _():
@@ -341,6 +360,15 @@
     lax.fori_loop(1, n, q_start, 0)
     qbuf[me] = pbuf[me]
 
+    lax.fori_loop(half, nz, bc_wait, 0)
+    for q in range(batch * chunks):
+        lanes = slice(q * CHUNK, (q + 1) * CHUNK)
+        b_t = bcall[0:half, :, lanes].reshape(STATE, CHUNK)
+        c_t = bcall[half:nz, :, lanes].reshape(STATE, CHUNK)
+        scores = dot(c_t, b_t, TN)
+        lhs[q, :, 0:CHUNK] = jnp.where(causal, scores, 0.0).astype(BF16)
+        lhs[q, :, CHUNK:] = jnp.transpose(c_t.astype(F32)).astype(BF16)
+
     def q_wait(d, carry):
         q_copy(lax.rem(me + d, n), me).wait_recv()
         return carry
@@ -350,7 +378,8 @@
     ones = jnp.ones((8, inner), BF16)
     picked = lax.broadcasted_iota(jnp.int32, (8, CHUNK), 0)
     squares = jnp.zeros((8, CHUNK), F32)
-    gains = gain[...]
+    loads[10].wait()
+    gains = gain[...].reshape(1, inner)
     for b in range(batch):
         entering = qbuf[b * per_batch : (b + 1) * per_batch].astype(F32).reshape(STATE, inner)
         for c in range(chunks):
@@ -433,21 +462,25 @@
     chunks = batch * length // CHUNK
     rows = batch * (length + HALO)
     piece = batch * STATE // n
-    hbm = pl.BlockSpec(memory_space=pl.ANY)
+    hbm = pl.BlockSpec(memory_space=pltpu.HBM)
     vmem = pl.BlockSpec(memory_space=pltpu.VMEM)
     dma = pltpu.SemaphoreType.DMA
     return pl.pallas_call(
         functools.partial(kernel, n, nz, batch, length, inner, heads),
         out_shape=jax.ShapeDtypeStruct((batch, length, inner), BF16),
-        in_specs=[hbm] * 5 + [vmem] * 5,
+        in_specs=[hbm] * 10,
         out_specs=vmem,
         scratch_shapes=[
+            pltpu.VMEM(value_conv.shape, F32),
+            pltpu.VMEM(bc_conv.shape, F32),
+            pltpu.VMEM((1, heads), F32),
+            pltpu.VMEM((1, heads), F32),
+            pltpu.VMEM((inner,), F32),
             pltpu.VMEM((rows, width), BF16),
             pltpu.VMEM((width, 2 * inner), BF16),
-            pltpu.VMEM((width, nbc), BF16),
-            pltpu.VMEM((width, heads), BF16),
-            pltpu.VMEM((width, 256), BF16),
-            pltpu.VMEM((rows, 256), F32),
+            pltpu.VMEM((heads, width), BF16),
+            pltpu.VMEM((nbc + 16, width), BF16),
+            pltpu.VMEM((rows, nbc + 16), F32),
             pltpu.VMEM((rows, 2 * inner), F32),
             pltpu.VMEM((chunks, CHUNK, inner), BF16),
             pltpu.VMEM((chunks, CHUNK, CHUNK + STATE), BF16),
@@ -466,7 +499,7 @@
             pltpu.VMEM((128, inner), F32),
             pltpu.VMEM((chunks, 32, CHUNK), BF16),
             pltpu.VMEM((chunks, 32, CHUNK), BF16),
-            dma((6,)),
+            dma((11,)),
             dma((batch,)), dma((batch,)),
             dma((nz,)), dma((nz,)),
             dma((n,)), dma((n,)),
@@ -475,11 +508,16 @@
             dma((nz,)), dma((nz,)),
         ],
         compiler_params=pltpu.CompilerParams(
-            collective_id=0, has_side_effects=True, vmem_limit_bytes=60 * 1024 * 1024
+            collective_id=0, has_side_effects=True, vmem_limit_bytes=52 * 1024 * 1024
         ),
     )(
-        hidden_in, gate_proj, value_proj, bc_proj, step_proj, value_conv, bc_conv,
-        step_bias.reshape(1, heads), log_rate.reshape(1, heads), norm_gain.reshape(1, inner),
+        *(
+            pltpu.with_memory_space_constraint(x, pltpu.HBM)
+            for x in (
+                hidden_in, gate_proj, value_proj, bc_proj.T, step_proj.T, value_conv, bc_conv,
+                step_bias.reshape(1, heads), log_rate.reshape(1, heads), norm_gain,
+            )
+        )
     )
 
 

time: 60.5 us -> 52 us (0.86)
  local copies, waits for them, and re-layouts: 7.8 us -> 1.06 us
  Pallas kernels: 52.4 us -> 50.9 us
    unnamed x3 -> x1, local copies, waits for them, and re-layouts: 6.52 us -> 1.06 us
    pallas_call x1, Pallas kernels: 52.4 us -> 50.9 us  [on_device(): pl.pallas_call(functools.partial(kernel, n, nz, batch, length, inner, hea...]
    reshape x1 -> x0, local copies, waits for them, and re-layouts: 1.28 us -> none  [on_device(): norm_gain.reshape(1, inner)]
where the time goes in v2:
time: 52 us
  Pallas kernels  50.9 us (98%)
  local copies, waits for them, and re-layouts  1.06 us (2%)
    pallas_call x1, Pallas kernels, on_device(): pl.pallas_call(functools.partial(kernel, n, nz, batch, length, inner, hea...  50.9 us
    unnamed x1, local copies, waits for them, and re-layouts  1.06 us

profile of v2, /device:TPU:1, one launch (start us, length us, event | category | flops | bytes accessed | tf_op | source)
XLA Modules:
  0.0 52.0 jit_solution(11768453954184701859)
XLA Ops:
  0.0 50.9 %shard_map.100 = bf16[2,512,640]{2,1,0:T(8,128)(2,1)S(1)} custom-call(bf16[2,512,2560]{2,1,0:T(8,128)(2,1)} %hid_in.1, bf16[2560,640]{1,0:T(8,128)(2,1)} %gate_in.1, bf16[2560,640]{1,0:T(8,128)(2,1)} %value_in.1, bf16[32,2560]{1,0:T(8,128)(2,1)} %bitcast.4, bf16[10,2560]{1,0:T(8,128)(2,1)} %bitcast.5, f32[4,640]{1,0:T(4,128)} %vconv_in.1, ...), custom_call_target="tpu_custom_call" | custom-call | tf_op jit(solution)/shard_map/pallas_call | solution.py:468
  50.9 1.1 %copy.12 = bf16[2,512,640]{2,1,0:T(8,128)(2,1)} copy(bf16[2,512,640]{2,1,0:T(8,128)(2,1)S(1)} %shard_map.100) | data formatting | bytes 2621440

commit v3 on v2

--- a/solution.py
+++ b/solution.py
@@ -13,6 +13,7 @@
 HEAD_DIM = 64
 STATE = 128
 CONV = 4
+EARLY_GATE = True
 HALO = 16
 CHUNK = 128
 EPSILON = 1e-05
@@ -31,6 +32,17 @@
     return jnp.concatenate([high, low], axis=0)
 
 
+def bulk(view, send_sem, recv_sem, device_id):
+    return pltpu.make_async_remote_copy(
+        src_ref=view,
+        dst_ref=view,
+        send_sem=send_sem,
+        recv_sem=recv_sem,
+        device_id=device_id,
+        device_id_type=MESH,
+    )
+
+
 def silu(x):
     half = 0.5 * x
     return half * jnp.tanh(half) + half
@@ -47,9 +59,9 @@
     n, nz, batch, length, inner, heads,
     hid_in, gate_in, value_in, bc_in, step_in, vconv_in, bconv_in, bias_in, rate_in, gain_in,
     out,
-    vconv, bconv, bias, rate, gain, hid, wcat, stw, wsm, small, pre, xp, lhs, tbuf, bct, bcall, dsend, dall, dexp,
+    vconv, bconv, bias, rate, gain, hid, wcat, stw, wsm, pre, xp, lhs, tbuf, bct, bcall, edget, edgeall, brows, crows, dsend, dall, dexp,
     sbuf, rbuf, pbuf, qbuf, sssend, ssall, rowx, e1t, e2t,
-    load_sem, halo_s, halo_r, bc_s, bc_r, d_s, d_r, p_s, p_r, q_s, q_r, ss_s, ss_r,
+    load_sem, halo_s, halo_r, bc_s, bc_r, edge_s, edge_r, d_s, d_r, p_s, p_r, q_s, q_r, ss_s, ss_r,
 ):
     me = lax.axis_index("seq")
     z = lax.axis_index("tp")
@@ -57,7 +69,9 @@
     chunks = length // CHUNK
     piece = batch * STATE // n
     per_batch = n // batch
-    nbc = bct.shape[0]
+    nbc = bct.shape[1]
+    half = nz // 2
+    next_seq, next_tp = {"seq": lax.rem(me + 1, n)}, {"tp": lax.rem(z + 1, nz)}
     width = hid.shape[1]
 
     loads = []
@@ -107,10 +121,14 @@
     wsm[nbc : nbc + heads, :] = stw[...]
     wsm[nbc + heads : nbc + 16, :] = jnp.zeros((16 - heads, width), BF16)
 
+    raws = []
+
     def project_small(b):
         loads[b].wait()
         rows = pl.ds(b * step_rows + HALO, length)
-        small[rows, :] = dot(hid[rows, :], wsm[...], NT)
+        both = jnp.transpose(dot(hid[rows, :], wsm[...], NT))
+        bct[b] = both[0:nbc].astype(BF16)
+        raws.append(both[nbc : nbc + 16])
 
     project_small(0)
     pl.semaphore_wait(barrier, n - 1 + nz - 1)
@@ -137,8 +155,29 @@
         for b in range(batch):
             hid[pl.ds(b * step_rows, HALO), :] = jnp.zeros((HALO, width), BF16)
 
+    def bc_copy(source, target, b):
+        return pltpu.make_async_remote_copy(
+            src_ref=bct.at[b],
+            dst_ref=bcall.at[source, b],
+            send_sem=bc_s,
+            recv_sem=bc_r.at[source // half],
+            device_id={"tp": target},
+            device_id_type=MESH,
+        )
+
+    def send_bc(b):
+        def bc_start(d, carry):
+            bc_copy(z, lax.rem(z + d, nz), b).start()
+            return carry
+
+        lax.fori_loop(1, nz, bc_start, 0)
+        bcall[z, b] = bct[b]
+
+    send_bc(0)
+
     for b in range(1, batch):
         project_small(b)
+        send_bc(b)
 
     loads[8].wait()
     loads[9].wait()
@@ -149,8 +188,7 @@
     live = lax.broadcasted_iota(jnp.int32, (16, length), 0) < heads
     steps, parts = [], []
     for b in range(batch):
-        raw = jnp.transpose(small[pl.ds(b * step_rows + HALO, length), nbc : nbc + 16])
-        raw = jnp.where(live, raw + bias_col, 0.0)
+        raw = jnp.where(live, raws[b] + bias_col, 0.0)
         size = jnp.maximum(raw, 0.0) + jnp.log1p(jnp.exp(-jnp.abs(raw)))
         size = jnp.where(live, size, 0.0)
         steps.append(size)
@@ -185,8 +223,8 @@
         return pltpu.make_async_remote_copy(
             src_ref=dsend.at[target // per_batch],
             dst_ref=dall.at[source],
-            send_sem=d_s.at[target],
-            recv_sem=d_r.at[source],
+            send_sem=d_s,
+            recv_sem=d_r,
             device_id={"seq": target},
             device_id_type=MESH,
         )
@@ -197,6 +235,20 @@
 
     lax.fori_loop(1, n, d_start, 0)
     dall[me] = dsend[me // per_batch]
+
+    loads[5].wait()
+    tiles = 2 * inner // 256
+    value_tiles = -(-inner // 256)
+
+    def project_gate(t, carry):
+        columns_at = pl.ds(pl.multiple_of(t * 256, 256), 256)
+        for b in range(batch):
+            rows = pl.ds(b * step_rows + HALO, length)
+            pre[rows, columns_at] = dot(hid[rows, :], wcat[:, columns_at])
+        return carry
+
+    if EARLY_GATE:
+        project_gate(tiles - 1, 0)
 
     @pl.when(me > 0)
     def _():
@@ -204,45 +256,31 @@
             halo_copy(b, following).wait_recv()
 
     edge = dot(
+        wsm[0:nbc, :],
         jnp.concatenate([hid[pl.ds(b * step_rows, HALO), :] for b in range(batch)], axis=0),
-        wsm[...],
         NT,
     )
-    for b in range(batch):
-        small[pl.ds(b * step_rows, HALO), :] = edge[b * HALO : (b + 1) * HALO]
-
-    loads[7].wait()
-    taps = pltpu.roll(
-        jnp.concatenate([bconv[...], jnp.zeros((8 - CONV, 2 * STATE), F32)], axis=0),
-        lax.rem(2 * STATE - z * nbc, 2 * STATE),
-        1,
-    )[:, 0:nbc]
-    for b in range(batch):
-        base = b * step_rows
-        window = small[pl.ds(base + 8, length + 8), 0:nbc].astype(BF16).astype(F32)
-        rows = conv_silu(window, taps, length)
-        bct[:, b * length : (b + 1) * length] = jnp.transpose(rows).astype(BF16)
-    bcall[z] = bct[...]
-
-    def bc_copy(source, target):
-        return pltpu.make_async_remote_copy(
-            src_ref=bct,
-            dst_ref=bcall.at[source],
-            send_sem=bc_s.at[target],
-            recv_sem=bc_r.at[source],
+    edge = jnp.concatenate([edge, jnp.zeros((nbc, 128 - batch * HALO), F32)], axis=1)
+    edget[...] = edge.astype(BF16)
+    edgeall[z] = edge.astype(BF16)
+
+    def edge_copy(source, target):
+        return pltpu.make_async_remote_copy(
+            src_ref=edget,
+            dst_ref=edgeall.at[source],
+            send_sem=edge_s,
+            recv_sem=edge_r,
             device_id={"tp": target},
             device_id_type=MESH,
         )
 
-    def bc_start(d, carry):
-        bc_copy(z, lax.rem(z + d, nz)).start()
-        return carry
-
-    half = nz // 2
-    lax.fori_loop(1, nz, bc_start, 0)
+    def edge_start(d, carry):
+        edge_copy(z, lax.rem(z + d, nz)).start()
+        return carry
+
+    lax.fori_loop(1, nz, edge_start, 0)
 
     loads[4].wait()
-    loads[5].wait()
 
     def project(t, carry):
         columns_at = pl.ds(pl.multiple_of(t * 256, 256), 256)
@@ -253,7 +291,6 @@
             )
         return carry
 
-    value_tiles = -(-inner // 256)
     lax.fori_loop(0, value_tiles, project, 0)
 
     loads[6].wait()
@@ -267,24 +304,39 @@
 
     lax.fori_loop(0, batch * chunks, values_of, 0)
 
-    lax.fori_loop(value_tiles, 2 * inner // 256, project, 0)
-
-    def gates_of(q, carry):
-        base = pl.multiple_of((q // chunks) * step_rows + lax.rem(q, chunks) * CHUNK + HALO, 8)
-        at = pl.ds(base, CHUNK)
-        pre[at, inner:] = silu(pre[at, inner:]) * dot(e2t[q], spread, TN)
-        return carry
-
-    lax.fori_loop(0, batch * chunks, gates_of, 0)
-
-    def bc_wait(s, carry):
-        @pl.when(s != z)
-        def _():
-            bc_copy(s, z).wait_recv()
-
-        return carry
-
-    lax.fori_loop(0, half, bc_wait, 0)
+    def bc_wait(group):
+        blocks = [(z // half != group, half)]
+        if half > 1:
+            blocks.append((z // half == group, half - 1))
+        for condition, count in blocks:
+
+            @pl.when(condition)
+            def _(count=count):
+                bulk(bcall.at[pl.ds(0, count)], bc_s, bc_r.at[group], next_tp).wait_recv()
+
+    loads[7].wait()
+    taps = jnp.transpose(
+        jnp.concatenate([bconv[...], jnp.zeros((8 - CONV, 2 * STATE), F32)], axis=0)
+    )
+
+    def conv_rows(first, b):
+        sources = slice(first * half, (first + 1) * half)
+        tail = edgeall[sources].reshape(STATE, 128).astype(F32)
+        tail = pltpu.roll(tail, 128 - (b + 1) * HALO, 1)
+        body = bcall[sources, b].reshape(STATE, length).astype(F32)
+        whole = jnp.concatenate([tail, body], axis=1)
+        weights = taps[first * STATE : (first + 1) * STATE]
+        total = weights[:, CONV - 1 : CONV] * body
+        for k in range(CONV - 1):
+            shifted = pltpu.roll(whole, CONV - 1 - k, 1)[:, 128:]
+            total = total + weights[:, k : k + 1] * shifted
+        return silu(total).astype(BF16)
+
+    bc_wait(0)
+    bulk(edgeall.at[pl.ds(0, nz - 1)], edge_s, edge_r, next_tp).wait_recv()
+
+    for b in range(batch):
+        brows[:, b * length : (b + 1) * length] = conv_rows(0, b)
 
     causal = (
         lax.broadcasted_iota(jnp.int32, (CHUNK, CHUNK), 0)
@@ -295,7 +347,7 @@
         for c in range(chunks):
             q = b * chunks + c
             lanes = slice(b * length + c * CHUNK, b * length + (c + 1) * CHUNK)
-            rows = bcall[0:half, :, lanes].reshape(STATE, CHUNK)
+            rows = brows[:, lanes]
             if c:
                 tbuf[q] = state * rowx[q : q + 1]
                 state = state * rowx[8 + q : 9 + q]
@@ -311,8 +363,8 @@
         return pltpu.make_async_remote_copy(
             src_ref=sbuf.at[target],
             dst_ref=rbuf.at[source],
-            send_sem=p_s.at[target],
-            recv_sem=p_r.at[source],
+            send_sem=p_s,
+            recv_sem=p_r,
             device_id={"seq": target},
             device_id_type=MESH,
         )
@@ -323,57 +375,62 @@
 
     lax.fori_loop(1, n, p_start, 0)
 
-    def d_wait(d, carry):
-        d_copy(lax.rem(me + d, n), me).wait_recv()
-        return carry
-
-    lax.fori_loop(1, n, d_wait, 0)
+    lax.fori_loop(value_tiles, tiles - 1 if EARLY_GATE else tiles, project_gate, 0)
+
+    def gates_of(q, carry):
+        base = pl.multiple_of((q // chunks) * step_rows + lax.rem(q, chunks) * CHUNK + HALO, 8)
+        at = pl.ds(base, CHUNK)
+        pre[at, inner:] = silu(pre[at, inner:]) * dot(e2t[q], spread, TN)
+        return carry
+
+    lax.fori_loop(0, batch * chunks, gates_of, 0)
+
+    bulk(dall.at[pl.ds(0, n - 1)], d_s, d_r, next_seq).wait_recv()
     decays = dall[...].reshape(n * 8, 128)[:, 0:16]
     high = decays.astype(BF16)
     low = (decays - high.astype(F32)).astype(BF16)
     dexp[...] = (dot(high, spread[0:16]) + dot(low, spread[0:16])).reshape(n, 8, inner)
 
-    def scan_step(i, prefix):
-        @pl.when(i != me)
-        def _():
-            p_copy(i, me).wait_recv()
-
-        pbuf[i] = prefix.astype(BF16)
-        return dexp[i, 0:1, :] * prefix + rbuf[i].astype(F32)
-
-    lax.fori_loop(0, n, scan_step, jnp.zeros((piece, inner), F32))
-
-    def q_copy(source, target):
-        return pltpu.make_async_remote_copy(
-            src_ref=pbuf.at[target],
-            dst_ref=qbuf.at[source],
-            send_sem=q_s.at[target],
-            recv_sem=q_r.at[source],
-            device_id={"seq": target},
-            device_id_type=MESH,
-        )
-
-    def q_start(d, carry):
-        q_copy(me, lax.rem(me + d, n)).start()
-        return carry
-
-    lax.fori_loop(1, n, q_start, 0)
-    qbuf[me] = pbuf[me]
-
-    lax.fori_loop(half, nz, bc_wait, 0)
+    bc_wait(1)
+    for b in range(batch):
+        crows[:, b * length : (b + 1) * length] = conv_rows(1, b)
     for q in range(batch * chunks):
         lanes = slice(q * CHUNK, (q + 1) * CHUNK)
-        b_t = bcall[0:half, :, lanes].reshape(STATE, CHUNK)
-        c_t = bcall[half:nz, :, lanes].reshape(STATE, CHUNK)
+        b_t = brows[:, lanes]
+        c_t = crows[:, lanes]
         scores = dot(c_t, b_t, TN)
         lhs[q, :, 0:CHUNK] = jnp.where(causal, scores, 0.0).astype(BF16)
         lhs[q, :, CHUNK:] = jnp.transpose(c_t.astype(F32)).astype(BF16)
 
-    def q_wait(d, carry):
-        q_copy(lax.rem(me + d, n), me).wait_recv()
-        return carry
-
-    lax.fori_loop(1, n, q_wait, 0)
+    bulk(rbuf.at[pl.ds(0, n - 1)], p_s, p_r, next_seq).wait_recv()
+
+    def scan_step(i, prefix):
+        pbuf[i] = prefix.astype(BF16)
+        return dexp[i, 0:1, :] * prefix + rbuf[i].astype(F32)
+
+    lax.fori_loop(0, n, scan_step, jnp.zeros((piece, inner), F32))
+
+    def q_copy(source, target):
+        return pltpu.make_async_remote_copy(
+            src_ref=pbuf.at[target],
+            dst_ref=qbuf.at[source],
+            send_sem=q_s,
+            recv_sem=q_r,
+            device_id={"seq": target},
+            device_id_type=MESH,
+        )
+
+    def q_start(d, carry):
+        q_copy(me, lax.rem(me + d, n)).start()
+        return carry
+
+    lax.fori_loop(1, n, q_start, 0)
+    qbuf[me] = pbuf[me]
+
+    bulk(dall.at[pl.ds(0, n - 1)], d_s, d_r, next_seq).wait_send()
+    bulk(rbuf.at[pl.ds(0, n - 1)], p_s, p_r, next_seq).wait_send()
+
+    bulk(qbuf.at[pl.ds(0, n - 1)], q_s, q_r, next_seq).wait_recv()
 
     ones = jnp.ones((8, inner), BF16)
     picked = lax.broadcasted_iota(jnp.int32, (8, CHUNK), 0)
@@ -397,8 +454,8 @@
         return pltpu.make_async_remote_copy(
             src_ref=sssend,
             dst_ref=ssall.at[source],
-            send_sem=ss_s.at[target],
-            recv_sem=ss_r.at[source],
+            send_sem=ss_s,
+            recv_sem=ss_r,
             device_id={"tp": target},
             device_id_type=MESH,
         )
@@ -410,16 +467,23 @@
     lax.fori_loop(1, nz, ss_start, 0)
     ssall[z] = squares
 
-    def ss_wait(d, carry):
-        ss_copy(lax.rem(z + d, nz), z).wait_recv()
-        return carry
-
-    lax.fori_loop(1, nz, ss_wait, 0)
+    @pl.when(me < n - 1)
+    def _():
+        for b in range(batch):
+            halo_copy(b, following).wait_send()
+
+    bulk(qbuf.at[pl.ds(0, n - 1)], q_s, q_r, next_seq).wait_send()
+    bulk(bcall.at[pl.ds(0, nz - 1)], bc_s, bc_r.at[0], next_tp).wait_send()
+    bulk(edgeall.at[pl.ds(0, nz - 1)], edge_s, edge_r, next_tp).wait_send()
+
+    bulk(ssall.at[pl.ds(0, nz - 1)], ss_s, ss_r, next_tp).wait_recv()
+
     whole = ssall[0]
     for s in range(1, nz):
         whole = whole + ssall[s]
     factor = lax.rsqrt(whole / (inner * nz) + EPSILON)
     wide = jnp.ones((16, 128), BF16)
+
     for b in range(batch):
         for c in range(chunks):
             q = b * chunks + c
@@ -431,26 +495,7 @@
                     pre[at, col : col + 128] * scale
                 ).astype(BF16)
 
-    @pl.when(me < n - 1)
-    def _():
-        for b in range(batch):
-            halo_copy(b, following).wait_send()
-
-    def seq_sent(d, carry):
-        other = lax.rem(me + d, n)
-        d_copy(me, other).wait_send()
-        p_copy(me, other).wait_send()
-        q_copy(me, other).wait_send()
-        return carry
-
-    def tp_sent(d, carry):
-        other = lax.rem(z + d, nz)
-        bc_copy(z, other).wait_send()
-        ss_copy(z, other).wait_send()
-        return carry
-
-    lax.fori_loop(1, n, seq_sent, 0)
-    lax.fori_loop(1, nz, tp_sent, 0)
+    bulk(ssall.at[pl.ds(0, nz - 1)], ss_s, ss_r, next_tp).wait_send()
 
 
 def on_device(
@@ -463,13 +508,12 @@
     rows = batch * (length + HALO)
     piece = batch * STATE // n
     hbm = pl.BlockSpec(memory_space=pltpu.HBM)
-    vmem = pl.BlockSpec(memory_space=pltpu.VMEM)
     dma = pltpu.SemaphoreType.DMA
     return pl.pallas_call(
         functools.partial(kernel, n, nz, batch, length, inner, heads),
         out_shape=jax.ShapeDtypeStruct((batch, length, inner), BF16),
         in_specs=[hbm] * 10,
-        out_specs=vmem,
+        out_specs=pl.BlockSpec(memory_space=pltpu.VMEM),
         scratch_shapes=[
             pltpu.VMEM(value_conv.shape, F32),
             pltpu.VMEM(bc_conv.shape, F32),
@@ -480,13 +524,16 @@
             pltpu.VMEM((width, 2 * inner), BF16),
             pltpu.VMEM((heads, width), BF16),
             pltpu.VMEM((nbc + 16, width), BF16),
-            pltpu.VMEM((rows, nbc + 16), F32),
             pltpu.VMEM((rows, 2 * inner), F32),
             pltpu.VMEM((chunks, CHUNK, inner), BF16),
             pltpu.VMEM((chunks, CHUNK, CHUNK + STATE), BF16),
             pltpu.VMEM((chunks, STATE, inner), F32),
-            pltpu.VMEM((nbc, batch * length), BF16),
-            pltpu.VMEM((nz, nbc, batch * length), BF16),
+            pltpu.VMEM((batch, nbc, length), BF16),
+            pltpu.VMEM((nz, batch, nbc, length), BF16),
+            pltpu.VMEM((nbc, 128), BF16),
+            pltpu.VMEM((nz, nbc, 128), BF16),
+            pltpu.VMEM((STATE, batch * length), BF16),
+            pltpu.VMEM((STATE, batch * length), BF16),
             pltpu.VMEM((batch, 8, 128), F32),
             pltpu.VMEM((n, 8, 128), F32),
             pltpu.VMEM((n, 8, inner), F32),
@@ -501,11 +548,12 @@
             pltpu.VMEM((chunks, 32, CHUNK), BF16),
             dma((11,)),
             dma((batch,)), dma((batch,)),
-            dma((nz,)), dma((nz,)),
-            dma((n,)), dma((n,)),
-            dma((n,)), dma((n,)),
-            dma((n,)), dma((n,)),
-            dma((nz,)), dma((nz,)),
+            dma, dma((2,)),
+            dma, dma,
+            dma, dma,
+            dma, dma,
+            dma, dma,
+            dma, dma,
         ],
         compiler_params=pltpu.CompilerParams(
             collective_id=0, has_side_effects=True, vmem_limit_bytes=52 * 1024 * 1024

time: 52 us -> 47.4 us (0.912)
  Pallas kernels: 50.9 us -> 46.3 us
    pallas_call x1, Pallas kernels: 50.9 us -> 46.3 us  [on_device(): pl.pallas_call(functools.partial(kernel, n, nz, batch, length, inner, hea...]
where the time goes in v3:
time: 47.4 us
  Pallas kernels  46.3 us (98%)
  local copies, waits for them, and re-layouts  1.06 us (2%)
    pallas_call x1, Pallas kernels, on_device(): pl.pallas_call(functools.partial(kernel, n, nz, batch, length, inner, hea...  46.3 us
    unnamed x1, local copies, waits for them, and re-layouts  1.06 us

profile of v3, /device:TPU:1, one launch (start us, length us, event | category | flops | bytes accessed | tf_op | source)
XLA Modules:
  0.0 47.4 jit_solution(2091565983924959334)
XLA Ops:
  0.0 46.3 %shard_map.100 = bf16[2,512,640]{2,1,0:T(8,128)(2,1)S(1)} custom-call(bf16[2,512,2560]{2,1,0:T(8,128)(2,1)} %hid_in.1, bf16[2560,640]{1,0:T(8,128)(2,1)} %gate_in.1, bf16[2560,640]{1,0:T(8,128)(2,1)} %value_in.1, bf16[32,2560]{1,0:T(8,128)(2,1)} %bitcast.4, bf16[10,2560]{1,0:T(8,128)(2,1)} %bitcast.5, f32[4,640]{1,0:T(4,128)} %vconv_in.1, ...), custom_call_target="tpu_custom_call" | custom-call | tf_op jit(solution)/shard_map/pallas_call | solution.py:512
  46.3 1.1 %copy.12 = bf16[2,512,640]{2,1,0:T(8,128)(2,1)} copy(bf16[2,512,640]{2,1,0:T(8,128)(2,1)S(1)} %shard_map.100) | data formatting | bytes 2621440

commit v4 on v3

--- a/solution.py
+++ b/solution.py
@@ -13,7 +13,6 @@
 HEAD_DIM = 64
 STATE = 128
 CONV = 4
-EARLY_GATE = True
 HALO = 16
 CHUNK = 128
 EPSILON = 1e-05
@@ -88,7 +87,7 @@
     tables = ((vconv_in, vconv), (bconv_in, bconv), (bias_in, bias), (rate_in, rate), (gain_in, gain))
     for k, (source, target) in enumerate(tables):
         loads.append(pltpu.make_async_copy(source, target, load_sem.at[6 + k]))
-    for k in (2, 3, 0, 1, 8, 9, 7, 6, 10, 4, 5):
+    for k in (2, 3, 0, 1, 8, 9, 7, 6, 10):
         loads[k].start()
 
     barrier = pltpu.get_barrier_semaphore()
@@ -125,6 +124,9 @@
 
     def project_small(b):
         loads[b].wait()
+        if b == 0:
+            loads[4].start()
+            loads[5].start()
         rows = pl.ds(b * step_rows + HALO, length)
         both = jnp.transpose(dot(hid[rows, :], wsm[...], NT))
         bct[b] = both[0:nbc].astype(BF16)
@@ -155,12 +157,14 @@
         for b in range(batch):
             hid[pl.ds(b * step_rows, HALO), :] = jnp.zeros((HALO, width), BF16)
 
-    def bc_copy(source, target, b):
+    relayed = nz == 8
+
+    def bc_copy(source, target, b, held=None):
         return pltpu.make_async_remote_copy(
-            src_ref=bct.at[b],
+            src_ref=bct.at[b] if held is None else held,
             dst_ref=bcall.at[source, b],
             send_sem=bc_s,
-            recv_sem=bc_r.at[source // half],
+            recv_sem=bc_r.at[b, source],
             device_id={"tp": target},
             device_id_type=MESH,
         )
@@ -170,8 +174,21 @@
             bc_copy(z, lax.rem(z + d, nz), b).start()
             return carry
 
-        lax.fori_loop(1, nz, bc_start, 0)
+        if relayed:
+            for d in (2, nz - 2, 1, nz - 1):
+                bc_start(d, 0)
+        else:
+            lax.fori_loop(1, nz, bc_start, 0)
         bcall[z, b] = bct[b]
+
+    def relay_bc(b):
+        for d in (2, nz - 2):
+            source = lax.rem(z + d, nz)
+            bc_copy(source, z, b).wait_recv()
+            back = 1 if d == nz - 2 else nz - 1
+            hops = (2 * back, back) if (b == 0) == (back == 1) else (back,)
+            for hop in hops:
+                bc_copy(source, lax.rem(z + hop, nz), b, bcall.at[source, b]).start()
 
     send_bc(0)
 
@@ -236,6 +253,7 @@
     lax.fori_loop(1, n, d_start, 0)
     dall[me] = dsend[me // per_batch]
 
+
     loads[5].wait()
     tiles = 2 * inner // 256
     value_tiles = -(-inner // 256)
@@ -246,9 +264,6 @@
             rows = pl.ds(b * step_rows + HALO, length)
             pre[rows, columns_at] = dot(hid[rows, :], wcat[:, columns_at])
         return carry
-
-    if EARLY_GATE:
-        project_gate(tiles - 1, 0)
 
     @pl.when(me > 0)
     def _():
@@ -291,28 +306,39 @@
             )
         return carry
 
-    lax.fori_loop(0, value_tiles, project, 0)
+    if relayed:
+        relay_bc(0)
+        lax.fori_loop(0, 1, project, 0)
+        relay_bc(1)
+        lax.fori_loop(1, value_tiles, project, 0)
+    else:
+        lax.fori_loop(0, value_tiles, project, 0)
 
     loads[6].wait()
     vtaps = vconv[...]
 
     def values_of(q, carry):
         base = pl.multiple_of((q // chunks) * step_rows + lax.rem(q, chunks) * CHUNK + 8, 8)
-        rows = conv_silu(pre[pl.ds(base, CHUNK + 8), 0:inner], vtaps, CHUNK)
-        xp[q] = (rows * dot(e1t[q], spread, TN)).astype(BF16)
+        scale = dot(e1t[q], spread, TN)
+        for col in range(0, inner, 128):
+            cols = slice(col, col + 128)
+            rows = conv_silu(pre[pl.ds(base, CHUNK + 8), cols], vtaps[:, cols], CHUNK)
+            xp[q, :, cols] = (rows * scale[:, cols]).astype(BF16)
         return carry
 
     lax.fori_loop(0, batch * chunks, values_of, 0)
 
     def bc_wait(group):
-        blocks = [(z // half != group, half)]
-        if half > 1:
-            blocks.append((z // half == group, half - 1))
-        for condition, count in blocks:
-
-            @pl.when(condition)
-            def _(count=count):
-                bulk(bcall.at[pl.ds(0, count)], bc_s, bc_r.at[group], next_tp).wait_recv()
+        for s in range(group * half, (group + 1) * half):
+            away = lax.rem(s + nz - z, nz)
+            missing = away != 0
+            if relayed:
+                missing &= (away != 2) & (away != nz - 2)
+
+            @pl.when(missing)
+            def _(s=s):
+                for b in range(batch):
+                    bc_copy(s, z, b).wait_recv()
 
     loads[7].wait()
     taps = jnp.transpose(
@@ -349,10 +375,10 @@
             lanes = slice(b * length + c * CHUNK, b * length + (c + 1) * CHUNK)
             rows = brows[:, lanes]
             if c:
-                tbuf[q] = state * rowx[q : q + 1]
+                tbuf[q] = (state * rowx[q : q + 1]).astype(BF16)
                 state = state * rowx[8 + q : 9 + q]
             else:
-                tbuf[q] = jnp.zeros((STATE, inner), F32)
+                tbuf[q] = jnp.zeros((STATE, inner), BF16)
             state = state + rowx[16 + q : 17 + q] * dot(rows, xp[q])
         sbuf[b * per_batch : (b + 1) * per_batch] = state.reshape(
             per_batch, piece, inner
@@ -375,15 +401,7 @@
 
     lax.fori_loop(1, n, p_start, 0)
 
-    lax.fori_loop(value_tiles, tiles - 1 if EARLY_GATE else tiles, project_gate, 0)
-
-    def gates_of(q, carry):
-        base = pl.multiple_of((q // chunks) * step_rows + lax.rem(q, chunks) * CHUNK + HALO, 8)
-        at = pl.ds(base, CHUNK)
-        pre[at, inner:] = silu(pre[at, inner:]) * dot(e2t[q], spread, TN)
-        return carry
-
-    lax.fori_loop(0, batch * chunks, gates_of, 0)
+    lax.fori_loop(value_tiles, tiles, project_gate, 0)
 
     bulk(dall.at[pl.ds(0, n - 1)], d_s, d_r, next_seq).wait_recv()
     decays = dall[...].reshape(n * 8, 128)[:, 0:16]
@@ -427,27 +445,47 @@
     lax.fori_loop(1, n, q_start, 0)
     qbuf[me] = pbuf[me]
 
+    def local_of(q, carry):
+        base = pl.multiple_of((q // chunks) * step_rows + lax.rem(q, chunks) * CHUNK + HALO, 8)
+        at = pl.ds(base, CHUNK)
+        scale = dot(e2t[q], spread, TN)
+        mixed = dot(lhs[q], jnp.concatenate([xp[q], tbuf[q]], axis=0))
+        which = lax.broadcasted_iota(jnp.int32, (8, inner), 0) == q
+        refs = jnp.sum(jnp.where(which, rowx[24:32, :], 0.0), axis=0, keepdims=True)
+        for col in range(0, inner, 128):
+            cols = slice(inner + col, inner + col + 128)
+            gate = silu(pre[at, cols]) * scale[:, col : col + 128]
+            pre[at, col : col + 128] = mixed[:, col : col + 128] * gate
+            pre[at, cols] = gate * refs[:, col : col + 128]
+        return carry
+
+    lax.fori_loop(0, batch * chunks, local_of, 0)
+
     bulk(dall.at[pl.ds(0, n - 1)], d_s, d_r, next_seq).wait_send()
     bulk(rbuf.at[pl.ds(0, n - 1)], p_s, p_r, next_seq).wait_send()
 
     bulk(qbuf.at[pl.ds(0, n - 1)], q_s, q_r, next_seq).wait_recv()
 
-    ones = jnp.ones((8, inner), BF16)
     picked = lax.broadcasted_iota(jnp.int32, (8, CHUNK), 0)
     squares = jnp.zeros((8, CHUNK), F32)
     loads[10].wait()
     gains = gain[...].reshape(1, inner)
     for b in range(batch):
-        entering = qbuf[b * per_batch : (b + 1) * per_batch].astype(F32).reshape(STATE, inner)
+        entering = qbuf[b * per_batch : (b + 1) * per_batch].astype(F32)
+        entering = entering.reshape(STATE, inner).astype(BF16)
+        at = pl.ds(b * step_rows + HALO, length)
+        readout = lhs[b * chunks : (b + 1) * chunks, :, CHUNK:].reshape(length, STATE)
+        sums = jnp.zeros((8, length), F32)
+        for col in range(0, inner, 256):
+            last = min(col + 256, inner)
+            gated = pre[at, col:last] + dot(readout, entering[:, col:last]) * pre[
+                at, inner + col : inner + last
+            ]
+            pre[at, col:last] = gated * gains[:, col:last]
+            sums += dot(jnp.ones((8, last - col), BF16), (gated * gated).astype(BF16), NT)
         for c in range(chunks):
-            q = b * chunks + c
-            state = (tbuf[q] + entering * rowx[24 + q : 25 + q]).astype(BF16)
-            at = pl.ds(b * step_rows + HALO + c * CHUNK, CHUNK)
-            mixed = dot(lhs[q], jnp.concatenate([xp[q], state], axis=0))
-            gated = mixed * pre[at, inner:]
-            pre[at, 0:inner] = gated * gains
-            sums = dot(ones, (gated * gated).astype(BF16), NT)
-            squares = jnp.where(picked == q, sums, squares)
+            part = sums[:, c * CHUNK : (c + 1) * CHUNK]
+            squares = jnp.where(picked == b * chunks + c, part, squares)
     sssend[...] = squares
 
     def ss_copy(source, target):
@@ -473,7 +511,7 @@
             halo_copy(b, following).wait_send()
 
     bulk(qbuf.at[pl.ds(0, n - 1)], q_s, q_r, next_seq).wait_send()
-    bulk(bcall.at[pl.ds(0, nz - 1)], bc_s, bc_r.at[0], next_tp).wait_send()
+    bulk(bcall.at[pl.ds(0, nz - 1)], bc_s, bc_r.at[0, 0], next_tp).wait_send()
     bulk(edgeall.at[pl.ds(0, nz - 1)], edge_s, edge_r, next_tp).wait_send()
 
     bulk(ssall.at[pl.ds(0, nz - 1)], ss_s, ss_r, next_tp).wait_recv()
@@ -527,7 +565,7 @@
             pltpu.VMEM((rows, 2 * inner), F32),
             pltpu.VMEM((chunks, CHUNK, inner), BF16),
             pltpu.VMEM((chunks, CHUNK, CHUNK + STATE), BF16),
-            pltpu.VMEM((chunks, STATE, inner), F32),
+            pltpu.VMEM((chunks, STATE, inner), BF16),
             pltpu.VMEM((batch, nbc, length), BF16),
             pltpu.VMEM((nz, batch, nbc, length), BF16),
             pltpu.VMEM((nbc, 128), BF16),
@@ -548,7 +586,7 @@
             pltpu.VMEM((chunks, 32, CHUNK), BF16),
             dma((11,)),
             dma((batch,)), dma((batch,)),
-            dma, dma((2,)),
+            dma, dma((batch, nz)),
             dma, dma,
             dma, dma,
             dma, dma,

time: 47.4 us -> 45.1 us (0.951)
  Pallas kernels: 46.3 us -> 43.9 us
    pallas_call x1, Pallas kernels: 46.3 us -> 43.9 us  [on_device(): pl.pallas_call(functools.partial(kernel, n, nz, batch, length, inner, hea...]
where the time goes in v4:
time: 45.1 us; the launch traced here: 45 us
  Pallas kernels  43.9 us (97%)
  local copies, waits for them, and re-layouts  1.06 us (2%)
    pallas_call x1, Pallas kernels, on_device(): pl.pallas_call(functools.partial(kernel, n, nz, batch, length, inner, hea...  43.9 us
    unnamed x1, local copies, waits for them, and re-layouts  1.06 us

profile of v4, /device:TPU:1, one launch (start us, length us, event | category | flops | bytes accessed | tf_op | source)
XLA Modules:
  0.0 45.0 jit_solution(9782257728026473005)
XLA Ops:
  0.0 43.9 %shard_map.100 = bf16[2,512,640]{2,1,0:T(8,128)(2,1)S(1)} custom-call(bf16[2,512,2560]{2,1,0:T(8,128)(2,1)} %hid_in.1, bf16[2560,640]{1,0:T(8,128)(2,1)} %gate_in.1, bf16[2560,640]{1,0:T(8,128)(2,1)} %value_in.1, bf16[32,2560]{1,0:T(8,128)(2,1)} %bitcast.4, bf16[10,2560]{1,0:T(8,128)(2,1)} %bitcast.5, f32[4,640]{1,0:T(4,128)} %vconv_in.1, ...), custom_call_target="tpu_custom_call" | custom-call | tf_op jit(solution)/shard_map/pallas_call | solution.py:550
  43.9 1.1 %copy.12 = bf16[2,512,640]{2,1,0:T(8,128)(2,1)} copy(bf16[2,512,640]{2,1,0:T(8,128)(2,1)S(1)} %shard_map.100) | data formatting | bytes 2621440

commit v5 on v4

--- a/solution.py
+++ b/solution.py
@@ -70,6 +70,7 @@
     per_batch = n // batch
     nbc = bct.shape[1]
     half = nz // 2
+
     next_seq, next_tp = {"seq": lax.rem(me + 1, n)}, {"tp": lax.rem(z + 1, nz)}
     width = hid.shape[1]
 
@@ -319,11 +320,8 @@
 
     def values_of(q, carry):
         base = pl.multiple_of((q // chunks) * step_rows + lax.rem(q, chunks) * CHUNK + 8, 8)
-        scale = dot(e1t[q], spread, TN)
-        for col in range(0, inner, 128):
-            cols = slice(col, col + 128)
-            rows = conv_silu(pre[pl.ds(base, CHUNK + 8), cols], vtaps[:, cols], CHUNK)
-            xp[q, :, cols] = (rows * scale[:, cols]).astype(BF16)
+        rows = conv_silu(pre[pl.ds(base, CHUNK + 8), 0:inner], vtaps, CHUNK)
+        xp[q] = (rows * dot(e1t[q], spread, TN)).astype(BF16)
         return carry
 
     lax.fori_loop(0, batch * chunks, values_of, 0)
@@ -399,7 +397,8 @@
         p_copy(me, lax.rem(me + d, n)).start()
         return carry
 
-    lax.fori_loop(1, n, p_start, 0)
+    for d in range(1, n):
+        p_start(d, 0)
 
     lax.fori_loop(value_tiles, tiles, project_gate, 0)
 
@@ -442,7 +441,8 @@
         q_copy(me, lax.rem(me + d, n)).start()
         return carry
 
-    lax.fori_loop(1, n, q_start, 0)
+    for d in range(1, n):
+        q_start(d, 0)
     qbuf[me] = pbuf[me]
 
     def local_of(q, carry):

time: 45.1 us -> 44.7 us (level)
  no operation moved by 1% of the time
where the time goes in v5:
time: 44.7 us
  Pallas kernels  43.6 us (98%)
  local copies, waits for them, and re-layouts  1.06 us (2%)
    pallas_call x1, Pallas kernels, on_device(): pl.pallas_call(functools.partial(kernel, n, nz, batch, length, inner, hea...  43.6 us
    unnamed x1, local copies, waits for them, and re-layouts  1.06 us

profile of v5, /device:TPU:1, one launch (start us, length us, event | category | flops | bytes accessed | tf_op | source)
XLA Modules:
  0.0 44.7 jit_solution(7047803083334754743)
XLA Ops:
  0.0 43.6 %shard_map.100 = bf16[2,512,640]{2,1,0:T(8,128)(2,1)S(1)} custom-call(bf16[2,512,2560]{2,1,0:T(8,128)(2,1)} %hid_in.1, bf16[2560,640]{1,0:T(8,128)(2,1)} %gate_in.1, bf16[2560,640]{1,0:T(8,128)(2,1)} %value_in.1, bf16[32,2560]{1,0:T(8,128)(2,1)} %bitcast.4, bf16[10,2560]{1,0:T(8,128)(2,1)} %bitcast.5, f32[4,640]{1,0:T(4,128)} %vconv_in.1, ...), custom_call_target="tpu_custom_call" | custom-call | tf_op jit(solution)/shard_map/pallas_call | solution.py:550
  43.6 1.1 %copy.12 = bf16[2,512,640]{2,1,0:T(8,128)(2,1)} copy(bf16[2,512,640]{2,1,0:T(8,128)(2,1)S(1)} %shard_map.100) | data formatting | bytes 2621440
